TPU v7x, 8 devices: a whole 2x2x1 slice. The times are simulated.
8 devices in a mesh: cp: 8 (over z, y, x, core).
Axes of the slice: x: 2, y: 2, z: 1, core: 2. Of those that a mesh axis runs over, the one named last changes fastest.
Arguments:
- x_in: bfloat16 [3, 4096, 2048], P(None, 'cp')
- grad_y: bfloat16 [3, 4096, 2048], P(None, 'cp')
- positions: int32 [3, 4096], P(None, 'cp')
- norm_gain: bfloat16 [2048], replicated
- w_query: bfloat16 [2048, 2048], replicated
- w_key: bfloat16 [2048, 1024], replicated
- w_value: bfloat16 [2048, 1024], replicated
- w_out: bfloat16 [2048, 2048], replicated
- q_gain: bfloat16 [128], replicated
- k_gain: bfloat16 [128], replicated
Outputs:
- output 1: bfloat16 [3, 4096, 2048], P(None, 'cp')
- output 2: bfloat16 [3, 4096, 2048], P(None, 'cp')
- output 3: float32 [2048], replicated
- output 4: float32 [2048, 2048], replicated
- output 5: float32 [2048, 1024], replicated
- output 6: float32 [2048, 1024], replicated
- output 7: float32 [2048, 2048], replicated
- output 8: float32 [128], replicated
- output 9: float32 [128], replicated
All inputs are finite; a program needn't handle non-finite values.
Results may differ from a plain program's by a relative error of at most 0.0178088.
Values are sent between devices in bfloat16 or wider.
A program may use at most 1 GiB of HBM per device.

v0:
```python
import jax
import jax.numpy as jnp
from jax import lax
from jax.experimental import pallas as pl
from jax.experimental.pallas import tpu as pltpu
from jax.sharding import PartitionSpec as P


SEQ_AXIS = 'cp'
ROPE_THETA = 1000000.0
EPSILON = 1e-6
MASK_VALUE = -1e30
LOG2E = 1.4426950408889634
HD = 128
BLK = 512
F32 = jnp.float32
BF16 = jnp.bfloat16
VMEM_LIMIT = 60 * 1024 * 1024


def dot_nn(a, b):
    return lax.dot_general(a, b, (((1,), (0,)), ((), ())), preferred_element_type=F32)


def dot_nt(a, b):
    return lax.dot_general(a, b, (((1,), (1,)), ((), ())), preferred_element_type=F32)


def prep(t, gain, cos, sin):
    r = lax.rsqrt(jnp.mean(t * t, axis=-1, keepdims=True) + EPSILON)
    normed = t * r * gain
    return normed * cos + pltpu.roll(normed, HD // 2, 1) * sin


def prep_back(d_rot, t, gain, cos, sin):
    d_norm = d_rot * cos - pltpu.roll(d_rot, HD // 2, 1) * sin
    r = lax.rsqrt(jnp.mean(t * t, axis=-1, keepdims=True) + EPSILON)
    d_gain = jnp.sum(d_norm * (t * r), axis=0, keepdims=True)
    scaled = d_norm * gain
    dot_mean = jnp.mean(scaled * t, axis=-1, keepdims=True)
    return r * scaled - t * (r * r * r * dot_mean), d_gain


def proj_kernel(n_ref, w_ref, cos_ref, sin_ref, qg_ref, kg_ref, q_ref, qt_ref, k_ref, kt_ref, v_ref, vt_ref, lin_ref):
    sub = BLK // 4
    for part in range(4):
        r = slice(part * sub, (part + 1) * sub)
        lin = dot_nn(n_ref[r, :], w_ref[...])
        lin_ref[r, :] = lin[:, :3 * HD]
        cos, sin = cos_ref[r, :], sin_ref[r, :]
        for h in range(2):
            q = prep(lin[:, h * HD:(h + 1) * HD], qg_ref[...], cos, sin)
            q_ref[r, h * HD:(h + 1) * HD] = q.astype(BF16)
            qt_ref[h * HD:(h + 1) * HD, r] = q.T.astype(BF16)
        k = prep(lin[:, 2 * HD:3 * HD], kg_ref[...], cos, sin)
        k_ref[r, :] = k.astype(BF16)
        kt_ref[:, r] = k.T.astype(BF16)
        v = lin[:, 3 * HD:]
        v_ref[r, :] = v.astype(BF16)
        vt_ref[:, r] = v.T.astype(BF16)


def project(n_all, w_own, cos, sin, qg, kg):
    toks = n_all.shape[0]
    full = lambda i: (0, 0)
    row = lambda i: (i, 0)
    col = lambda i: (0, i)
    sds = jax.ShapeDtypeStruct
    return pl.pallas_call(
        proj_kernel,
        grid=(toks // BLK,),
        in_specs=[pl.BlockSpec((BLK, n_all.shape[1]), row), pl.BlockSpec(w_own.shape, full),
                  pl.BlockSpec((BLK, HD), row), pl.BlockSpec((BLK, HD), row),
                  pl.BlockSpec((1, HD), full), pl.BlockSpec((1, HD), full)],
        out_specs=[pl.BlockSpec((BLK, 2 * HD), row), pl.BlockSpec((2 * HD, BLK), col),
                   pl.BlockSpec((BLK, HD), row), pl.BlockSpec((HD, BLK), col),
                   pl.BlockSpec((BLK, HD), row), pl.BlockSpec((HD, BLK), col),
                   pl.BlockSpec((BLK, 3 * HD), row)],
        out_shape=[sds((toks, 2 * HD), BF16), sds((2 * HD, toks), BF16), sds((toks, HD), BF16), sds((HD, toks), BF16),
                   sds((toks, HD), BF16), sds((HD, toks), BF16), sds((toks, 3 * HD), F32)],
        compiler_params=pltpu.CompilerParams(vmem_limit_bytes=VMEM_LIMIT),
        cost_estimate=pl.CostEstimate(flops=2 * toks * n_all.shape[1] * 4 * HD, bytes_accessed=30_000_000, transcendentals=0),
        name='proj',
    )(n_all, w_own, cos, sin, qg, kg)


def fwd_kernel(qt_ref, k_ref, vt_ref, o_ref, ot_ref, lse_ref, acc, m_s, l_s):
    i = pl.program_id(0)
    scale = HD ** -0.5 * LOG2E
    acc[...] = jnp.zeros_like(acc)
    m_s[...] = jnp.full_like(m_s, MASK_VALUE)
    l_s[...] = jnp.zeros_like(l_s)

    def step(j, masked):
        start = pl.multiple_of(j * BLK, BLK)
        k = k_ref[pl.ds(start, BLK), :]
        vt = vt_ref[:, pl.ds(start, BLK)]
        scores = [dot_nn(k, qt_ref[h * HD:(h + 1) * HD, :]) for h in range(2)]
        for h in range(2):
            s = scores[h]
            if masked:
                keys = lax.broadcasted_iota(jnp.int32, s.shape, 0)
                queries = lax.broadcasted_iota(jnp.int32, s.shape, 1)
                s = jnp.where(keys <= queries, s, MASK_VALUE)
            m_old = m_s[h:h + 1, :]
            m_new = jnp.maximum(m_old, jnp.max(s, axis=0, keepdims=True))
            p = jnp.exp2((s - m_new) * scale)
            alpha = jnp.exp2((m_old - m_new) * scale)
            m_s[h:h + 1, :] = m_new
            l_s[h:h + 1, :] = l_s[h:h + 1, :] * alpha + jnp.sum(p, axis=0, keepdims=True)
            rows = slice(h * HD, (h + 1) * HD)
            acc[rows, :] = acc[rows, :] * alpha + dot_nn(vt, p.astype(BF16))

    def body(j, carry):
        step(j, False)
        return carry

    lax.fori_loop(0, i, body, 0)
    step(i, True)
    for h in range(2):
        rows = slice(h * HD, (h + 1) * HD)
        l = l_s[h:h + 1, :]
        ot = acc[rows, :] / l
        ot_ref[rows, :] = ot
        lse_ref[h:h + 1, :] = m_s[h:h + 1, :] * scale + jnp.log2(l)
        o_ref[:, rows] = ot.T.astype(BF16)


def attend(qt, k, vt):
    toks = k.shape[0]
    full = lambda i: (0, 0)
    row = lambda i: (i, 0)
    col = lambda i: (0, i)
    sds = jax.ShapeDtypeStruct
    pairs = toks * toks // 2
    return pl.pallas_call(
        fwd_kernel,
        grid=(toks // BLK,),
        in_specs=[pl.BlockSpec((2 * HD, BLK), col), pl.BlockSpec((toks, HD), full), pl.BlockSpec((HD, toks), full)],
        out_specs=[pl.BlockSpec((BLK, 2 * HD), row), pl.BlockSpec((2 * HD, BLK), col), pl.BlockSpec((2, BLK), col)],
        out_shape=[sds((toks, 2 * HD), BF16), sds((2 * HD, toks), F32), sds((2, toks), F32)],
        scratch_shapes=[pltpu.VMEM((2 * HD, BLK), F32), pltpu.VMEM((2, BLK), F32), pltpu.VMEM((2, BLK), F32)],
        compiler_params=pltpu.CompilerParams(vmem_limit_bytes=VMEM_LIMIT),
        cost_estimate=pl.CostEstimate(flops=2 * pairs * 4 * HD * 2, bytes_accessed=10_000_000, transcendentals=2 * pairs),
        name='attend',
    )(qt, k, vt)


def bwd_kernel(q_ref, qt_ref, do_ref, ot_ref, lse_ref, k_ref, kt_ref, v_ref, lin_ref, cos_ref, sin_ref,
               qg_ref, kg_ref, drot_ref, dlin_ref, dqg_ref, dkg_ref, dqt, dk_s, dv_s, dot_ref, delta_ref):
    j = pl.program_id(0)
    n_blk = pl.num_programs(0)
    scale = HD ** -0.5
    scale2 = scale * LOG2E

    @pl.when(j == 0)
    def _():
        dqt[...] = jnp.zeros_like(dqt)
        dqg_ref[...] = jnp.zeros_like(dqg_ref)
        dkg_ref[...] = jnp.zeros_like(dkg_ref)

        def turn(i, carry):
            part = pl.ds(pl.multiple_of(i * BLK, BLK), BLK)
            for h in range(2):
                rows = slice(h * HD, (h + 1) * HD)
                dot = do_ref[part, rows].astype(F32).T
                dot_ref[rows, part] = dot.astype(BF16)
                delta_ref[h:h + 1, part] = jnp.sum(ot_ref[rows, part] * dot, axis=0, keepdims=True)
            return carry

        lax.fori_loop(0, n_blk, turn, 0)

    dk_s[...] = jnp.zeros_like(dk_s)
    dv_s[...] = jnp.zeros_like(dv_s)
    k = k_ref[...]
    kt = kt_ref[...]
    v = v_ref[...]

    def step(i, masked):
        start = pl.multiple_of(i * BLK, BLK)
        cols = pl.ds(start, BLK)
        for h in range(2):
            rows = slice(h * HD, (h + 1) * HD)
            s = dot_nn(k, qt_ref[rows, cols])
            p = jnp.exp2(s * scale2 - lse_ref[h:h + 1, cols])
            if masked:
                keys = lax.broadcasted_iota(jnp.int32, s.shape, 0)
                queries = lax.broadcasted_iota(jnp.int32, s.shape, 1)
                p = jnp.where(keys <= queries, p, 0.0)
            dp = dot_nn(v, dot_ref[rows, cols])
            ds = (p * (dp - delta_ref[h:h + 1, cols])).astype(BF16)
            dv_s[...] += dot_nn(p.astype(BF16), do_ref[cols, rows])
            dk_s[...] += dot_nn(ds, q_ref[cols, rows])
            dqt[rows, cols] += dot_nn(kt, ds)

    step(j, True)

    def body(i, carry):
        step(i, False)
        return carry

    lax.fori_loop(j + 1, n_blk, body, 0)

    cos, sin = cos_ref[...], sin_ref[...]
    mine = pl.ds(pl.multiple_of(j * BLK, BLK), BLK)
    for h in range(3):
        rows = slice(h * HD, (h + 1) * HD)
        d_rot = (dqt[rows, mine].T if h < 2 else dk_s[...]) * scale
        d_rot = d_rot.astype(BF16)
        drot_ref[:, rows] = d_rot
        gain = qg_ref[...] if h < 2 else kg_ref[...]
        d_lin, d_gain = prep_back(d_rot.astype(F32), lin_ref[:, rows], gain, cos, sin)
        dlin_ref[:, rows] = d_lin.astype(BF16)
        if h < 2:
            dqg_ref[...] += d_gain
        else:
            dkg_ref[...] += d_gain
    dv = dv_s[...].astype(BF16)
    drot_ref[:, 3 * HD:] = dv
    dlin_ref[:, 3 * HD:] = dv


def attend_back(q, qt, do, seq, ot, lse, k, kt, v, lin, cos, sin, qg, kg):
    toks = k.shape[0]
    full = lambda i: (0, 0)
    row = lambda i: (i, 0)
    col = lambda i: (0, i)
    sds = jax.ShapeDtypeStruct
    pairs = toks * toks // 2
    whole = lambda a: pl.BlockSpec(a.shape, full)
    return pl.pallas_call(
        bwd_kernel,
        grid=(toks // BLK,),
        in_specs=[whole(q), whole(qt), pl.BlockSpec((None, toks, 2 * HD), lambda i: (seq, 0, 0)), whole(ot), whole(lse),
                  pl.BlockSpec((BLK, HD), row), pl.BlockSpec((HD, BLK), col), pl.BlockSpec((BLK, HD), row),
                  pl.BlockSpec((BLK, 3 * HD), row), pl.BlockSpec((BLK, HD), row), pl.BlockSpec((BLK, HD), row),
                  pl.BlockSpec((1, HD), full), pl.BlockSpec((1, HD), full)],
        out_specs=[pl.BlockSpec((BLK, 4 * HD), row), pl.BlockSpec((BLK, 4 * HD), row),
                   pl.BlockSpec((1, HD), full), pl.BlockSpec((1, HD), full)],
        out_shape=[sds((toks, 4 * HD), BF16), sds((toks, 4 * HD), BF16), sds((1, HD), F32), sds((1, HD), F32)],
        scratch_shapes=[pltpu.VMEM((2 * HD, toks), F32), pltpu.VMEM((BLK, HD), F32), pltpu.VMEM((BLK, HD), F32),
                        pltpu.VMEM((2 * HD, toks), BF16), pltpu.VMEM((2, toks), F32)],
        compiler_params=pltpu.CompilerParams(vmem_limit_bytes=VMEM_LIMIT),
        cost_estimate=pl.CostEstimate(flops=2 * pairs * 10 * HD * 2, bytes_accessed=20_000_000, transcendentals=2 * pairs),
        name='attend_back',
    )(q, qt, do, ot, lse, k, kt, v, lin, cos, sin, qg, kg)


def lin_kernel(n_ref, wq_ref, wk_ref, lin_ref):
    w = jnp.concatenate([wq_ref[...], wk_ref[...]], axis=1)
    for t in range(n_ref.shape[0] // BLK):
        rows = slice(t * BLK, (t + 1) * BLK)
        lin_ref[0, rows, :] = dot_nn(n_ref[rows, :], w)


def own_lin(n_own, w_query, w_key):
    toks, dim = n_own.shape
    groups = w_key.shape[1] // HD
    return pl.pallas_call(
        lin_kernel,
        grid=(groups,),
        in_specs=[pl.BlockSpec((toks, dim), lambda g: (0, 0)), pl.BlockSpec((dim, 2 * HD), lambda g: (0, g)),
                  pl.BlockSpec((dim, HD), lambda g: (0, g))],
        out_specs=pl.BlockSpec((1, toks, 3 * HD), lambda g: (g, 0, 0)),
        out_shape=jax.ShapeDtypeStruct((groups, toks, 3 * HD), F32),
        compiler_params=pltpu.CompilerParams(vmem_limit_bytes=VMEM_LIMIT),
        cost_estimate=pl.CostEstimate(flops=2 * toks * dim * 3 * HD * groups, bytes_accessed=60_000_000, transcendentals=0),
        name='own_lin',
    )(n_own, w_query, w_key)


def gradx_kernel(drot_ref, lin_ref, wq_ref, wk_ref, wv_ref, cos_ref, sin_ref, qg_ref, kg_ref, x_ref, gy_ref, ng_ref,
                 *rest):
    gx_ref, dng_ref, acc = rest[-3:]
    g = pl.program_id(0)

    @pl.when(g == 0)
    def _():
        acc[...] = jnp.zeros_like(acc)

    cos, sin = cos_ref[...], sin_ref[...]
    parts = []
    for h in range(3):
        rows = slice(h * HD, (h + 1) * HD)
        gain = qg_ref[...] if h < 2 else kg_ref[...]
        d_lin, _ = prep_back(drot_ref[0, :, rows].astype(F32), lin_ref[0, :, rows], gain, cos, sin)
        parts.append(d_lin.astype(BF16))
    parts.append(drot_ref[0, :, 3 * HD:])
    w = jnp.concatenate([wq_ref[...], wk_ref[...], wv_ref[...]], axis=1)
    acc[...] += dot_nt(jnp.concatenate(parts, axis=1), w)

    @pl.when(g == pl.num_programs(0) - 1)
    def _():
        d_n = acc[...].astype(BF16).astype(F32)
        x = x_ref[0].astype(F32)
        r = lax.rsqrt(jnp.mean(x * x, axis=-1, keepdims=True) + EPSILON)
        dng_ref[...] = jnp.sum(d_n * (x * r), axis=0, keepdims=True)
        scaled = d_n * ng_ref[...]
        dot_mean = jnp.mean(scaled * x, axis=-1, keepdims=True)
        gx_ref[0] = (gy_ref[0].astype(F32) + r * scaled - x * (r * r * r * dot_mean)).astype(BF16)


def grad_tokens(drot, lin, seq, w_query, w_key, w_value, cos, sin, qg, kg, x, gy, ng, so_far):
    groups, toks, _ = drot.shape
    dim = x.shape[2]
    own = pl.BlockSpec((1, toks, dim), lambda g: (seq, 0, 0))
    extra = () if so_far is None else (so_far,)
    full = lambda g: (0, 0)
    col = lambda g: (0, g)
    return pl.pallas_call(
        gradx_kernel,
        grid=(groups,),
        in_specs=[pl.BlockSpec((1, toks, 4 * HD), lambda g: (g, 0, 0)), pl.BlockSpec((1, toks, 3 * HD), lambda g: (g, seq, 0)),
                  pl.BlockSpec((dim, 2 * HD), col), pl.BlockSpec((dim, HD), col), pl.BlockSpec((dim, HD), col),
                  pl.BlockSpec((toks, HD), full), pl.BlockSpec((toks, HD), full), pl.BlockSpec((1, HD), full),
                  pl.BlockSpec((1, HD), full), own, own,
                  pl.BlockSpec((1, dim), full)] + [pl.BlockSpec(memory_space=pl.ANY)] * len(extra),
        out_specs=[own, pl.BlockSpec((1, dim), full)],
        out_shape=[jax.ShapeDtypeStruct(x.shape, BF16), jax.ShapeDtypeStruct((1, dim), F32)],
        input_output_aliases={12: 0} if extra else {},
        scratch_shapes=[pltpu.VMEM((toks, dim), F32)],
        compiler_params=pltpu.CompilerParams(vmem_limit_bytes=VMEM_LIMIT),
        cost_estimate=pl.CostEstimate(flops=2 * toks * dim * 4 * HD * groups, bytes_accessed=40_000_000, transcendentals=0),
        name='grad_tokens',
    )(drot, lin, w_query, w_key, w_value, cos, sin, qg, kg, x, gy, ng, *extra)


def alloc(shape, dtype):
    return pl.pallas_call(lambda out_ref: None, out_specs=pl.BlockSpec(memory_space=pl.ANY),
                          out_shape=jax.ShapeDtypeStruct(shape, dtype), name='alloc')()


def rope_tables(positions):
    half_dim = HD // 2
    inv_freq = ROPE_THETA ** (-jnp.arange(half_dim, dtype=F32) / half_dim)
    angles = positions.astype(F32)[..., None] * inv_freq
    cos, sin = jnp.cos(angles), jnp.sin(angles)
    return jnp.concatenate([cos, cos], axis=-1), jnp.concatenate([-sin, sin], axis=-1)


def solution(mesh):
    n_dev = mesh.shape[SEQ_AXIS]
    tok_spec = P(None, SEQ_AXIS, None)
    pos_spec = P(None, SEQ_AXIS)

    def swap(x, dist):
        return lax.ppermute(x, SEQ_AXIS, [(d, d ^ dist) for d in range(n_dev)])

    def device_fn(x_in, grad_y, positions, norm_gain, w_query, w_key, w_value, w_out, q_gain, k_gain):
        n_batch, seq_dev, dim = x_in.shape
        me = lax.axis_index(SEQ_AXIS)
        seq_len = seq_dev * n_dev
        ng = norm_gain.astype(F32)[None]
        qg = q_gain.astype(F32)[None]
        kg = k_gain.astype(F32)[None]

        x32 = x_in.astype(F32)
        normed = (x32 * lax.rsqrt(jnp.mean(x32 * x32, axis=-1, keepdims=True) + EPSILON) * ng).astype(BF16)

        def after(values, *waits):
            return lax.optimization_barrier((values, waits))[0]

        pos_all = alloc((n_batch, seq_len), jnp.int32)
        for dist in range(n_dev):
            pos_all = lax.dynamic_update_slice(pos_all, swap(positions, dist) if dist else positions, (0, (me ^ dist) * seq_dev))
        normed = after(normed, pos_all)
        n_all = [lax.all_gather(normed[b], SEQ_AXIS, axis=0, tiled=True) for b in range(n_batch)]
        cos_all, sin_all = rope_tables(pos_all)
        cos_own, sin_own = rope_tables(positions)
        own_cols = lambda w, width: lax.dynamic_slice_in_dim(w, me * width, width, axis=1)
        w_own = jnp.concatenate([own_cols(w_query, 2 * HD), own_cols(w_key, HD), own_cols(w_value, HD)], axis=1)

        def col_block(a, dev):
            return lax.dynamic_slice_in_dim(a, dev * 2 * HD, 2 * HD, axis=1)

        def row_block(a, dev):
            return lax.dynamic_slice_in_dim(a, dev * seq_dev, seq_dev, axis=0)

        def exchange(src, cut, put, got, window):
            here, src = lax.optimization_barrier((me, src))
            blocks = [cut(src, here ^ dist) for dist in range(1, n_dev)]
            came = [swap(blk, dist) for dist, blk in enumerate(blocks, 1)]
            came = after([cut(src, here)] + came, window)
            for dist in range(n_dev):
                got = put(got, came[dist], me ^ dist)
            return got

        gy_cat = grad_y.reshape(n_batch * seq_dev, dim)
        d_attn = dot_nt(gy_cat, w_out).astype(BF16)
        n_first, cos_all, sin_all, _ = lax.optimization_barrier((n_all[0], cos_all, sin_all, d_attn))
        n_in = [n_first, n_all[1], n_all[2]]
        saved, outs = [], []
        for b in range(n_batch):
            q, qt, k, kt, v, vt, lin = project(n_in[b], w_own, cos_all[b], sin_all[b], qg, kg)
            o, ot, lse = attend(qt, k, vt)
            saved.append((ot, lse, q, qt, k, kt, v, lin))
            outs.append(o)
            if b == 0:
                lin_own = own_lin(after(normed, lse).reshape(n_batch * seq_dev, dim), w_query, w_key)
                n_in[1] = after(n_in[1], lin_own)

        put_do = lambda got, blk, dev: lax.dynamic_update_slice(got, blk.reshape(n_batch, seq_dev, 2 * HD), (0, dev * seq_dev, 0))
        do_src = after(d_attn, saved[1][1])
        do_all = exchange(do_src, col_block, put_do, alloc((n_batch, seq_len, 2 * HD), BF16), saved[2][1])

        def take_o(b, o_cat, window):
            put = lambda got, blk, dev: lax.dynamic_update_slice(got, blk, (b * seq_dev, dev * 2 * HD))
            return exchange(outs[b], row_block, put, o_cat, window)

        def take_drot(drot, window):
            put = lambda got, blk, dev: lax.dynamic_update_slice(got, blk[None], (dev, 0, 0))
            return exchange(drot, row_block, put, alloc((n_dev, seq_dev, 4 * HD), BF16), window)

        def back(b, waits):
            ot, lse, q, qt, k, kt, v, lin = saved[b]
            q = after(q, waits)
            drot, dlin, dqg, dkg = attend_back(q, qt, do_all, b, ot, lse, k, kt, v, lin, cos_all[b], sin_all[b], qg, kg)
            dw = lax.dot_general(n_all[b], dlin, (((0,), (0,)), ((), ())), preferred_element_type=F32)
            return drot, dqg, dkg, dw

        def to_tokens(b, got, so_far):
            return grad_tokens(got, lin_own, b, w_query, w_key, w_value, cos_own[b], sin_own[b], qg, kg,
                               x_in, grad_y, ng, so_far)

        o_cat = alloc((n_batch * seq_dev, n_dev * 2 * HD), BF16)
        o_cat = take_o(0, o_cat, saved[2][1])
        drot0, dqg0, dkg0, dw0 = back(0, ())
        o_cat = take_o(1, o_cat, drot0)
        o_cat = take_o(2, o_cat, drot0)
        part = lax.dot_general(o_cat, gy_cat, (((0,), (0,)), ((), ())), preferred_element_type=F32)
        grad_w_out = lax.psum_scatter(part, SEQ_AXIS, scatter_dimension=0, tiled=True)
        drot1, dqg1, dkg1, dw1 = back(1, (part, dw0))
        dw01 = dw0 + dw1
        y_out = (x32.reshape(n_batch * seq_dev, dim) + dot_nn(after(o_cat, dw01), w_out)).astype(BF16).reshape(x_in.shape)
        grad_w_out = lax.all_gather(after(grad_w_out, (y_out, dw01)), SEQ_AXIS, axis=0, tiled=True)
        got0 = take_drot(drot0, drot1)
        drot2, dqg2, dkg2, dw2 = back(2, (dw01, y_out))
        dw_sum = dw01 + dw2
        got1 = take_drot(drot1, drot2)
        grad_x, dng0 = to_tokens(0, after(got0, dw_sum), None)
        grad_x, dng1 = to_tokens(1, got1, grad_x)
        grad_x, dng2 = to_tokens(2, take_drot(drot2, grad_x), grad_x)
        dng_sum, dqg_sum, dkg_sum = dng0 + dng1 + dng2, dqg0 + dqg1 + dqg2, dkg0 + dkg1 + dkg2

        def gather_cols(own):
            return jnp.moveaxis(lax.all_gather(own, SEQ_AXIS, axis=0), 0, 1).reshape(dim, -1)

        dw_sum, grad_w_out = lax.optimization_barrier((dw_sum, grad_w_out))
        grad_w_query = gather_cols(dw_sum[:, :2 * HD])
        dw_kv = lax.all_gather(after(dw_sum[:, 2 * HD:], dng0), SEQ_AXIS, axis=0)
        grad_w_key = jnp.moveaxis(dw_kv[:, :, :HD], 0, 1).reshape(dim, -1)
        grad_w_value = jnp.moveaxis(dw_kv[:, :, HD:], 0, 1).reshape(dim, -1)

        small = jnp.concatenate([dng_sum, dqg_sum, dkg_sum], axis=1)
        for dist in (1, 2, 4):
            small = small + swap(small, dist)
        small = small[0]
        return (y_out, grad_x, small[:dim], grad_w_query, grad_w_key, grad_w_value, grad_w_out,
                small[dim:dim + HD], small[dim + HD:])

    in_specs = (tok_spec, tok_spec, pos_spec, P(), P(), P(), P(), P(), P(), P())
    out_specs = (tok_spec, tok_spec, P(), P(), P(), P(), P(), P(), P())
    return jax.shard_map(device_fn, mesh=mesh, in_specs=in_specs, out_specs=out_specs, check_vma=False)
```

profile of v0, /device:TPU:0, one launch (start us, length us, event | category | flops | bytes accessed | tf_op | source)
XLA Modules:
  0.0 1135.5 jit_solution(1009959232078124699)
XLA Ops:
  8.1 2.5 collective-permute-start.1
  13.1 4.1 multiply_reduce_fusion
  17.3 7.0 multiply_convert_fusion
  24.9 2.6 collective-permute-start.5
  31.5 5.8 fusion.17
  41.6 2.3 constant_dynamic-slice_fusion.56
  45.5 17.4 %convolution_convert_fusion = bf16[1536,2048]{1,0:T(8,128)(2,1)} fusion(bf16[1536,2048]{1,0:T(8,128)(2,1)S(1)} %bitcast.138, bf16[2048,2048]{1,0:T(8,128)(2,1)} %param.17), kind=kOutput, calls=%fused_computation.10 | convolution fusion | flops 12888047616 | bytes 20971520 | tf_op jit(solution)/shard_map/dot_general | solution.py:26
  62.8 22.3 %fusion.1 = (f32[3,4096,64]{2,1,0:T(8,128)S(1)}, f32[3,4096,64]{2,1,0:T(8,128)S(1)}, f32[3,4096,64]{2,1,0:T(8,128)S(1)}) fusion(f32[64]{0:T(128)S(1)} %multiply_power_fusion, f32[3,4096]{1,0:T(4,128)S(1)} %convert_element_type.26), kind=kLoop, calls=%fused_computation.22 | loop fusion | flops 1572864 | bytes 9486592 | tf_op jit(solution)/shard_map/neg | solution.py:338
  85.2 6.4 pad_maximum_fusion
  91.6 29.2 %all-gather.14.cloned.1.call-done = bf16[1,4096,2048]{2,1,0:T(8,128)(2,1)} async-done(((bf16[1,512,2048]{2,1,0:T(8,128)(2,1)}), bf16[1,4096,2048]{2,1,0:T(8,128)(2,1)}) %all-gather.14.cloned.1.call-update) | async-done | bytes 16777232 | tf_op jit(solution)/shard_map/all_gather | solution.py:367
  120.7 6.3 slice_bitcast_fusion.2
  127.0 3.1 slice_bitcast_fusion.3
  130.1 19.5 %proj.3 = (bf16[4096,256]{1,0:T(8,128)(2,1)}, bf16[256,4096]{1,0:T(8,128)(2,1)}, bf16[4096,128]{1,0:T(8,128)(2,1)}, bf16[128,4096]{1,0:T(8,128)(2,1)}, bf16[4096...) custom-call(bf16[4096,2048]{1,0:T(8,128)(2,1)} %bitcast.159, ...), custom_call_target="tpu_custom_call" | custom-call | flops 8589934592 | bytes 30000000 | tf_op jit(solution)/shard_map/proj/pallas_call | solution.py:69
  149.6 39.6 %attend.3 = (bf16[4096,256]{1,0:T(8,128)(2,1)}, f32[256,4096]{1,0:T(8,128)}, f32[2,4096]{1,0:T(2,128)}) custom-call(bf16[256,4096]{1,0:T(8,128)(2,1)} %get-tuple-element.146.qt_ref, bf16[4096,128]{1,0:T(8,128)(2,1)} %get-tuple-element.147.k_ref, bf16[128,4096]{1,0:T(8,128)(2,1)} %get-tuple-element.148.vt_ref), custom_call_target="tpu_custom_call" | custom-call | flops 17179869184 | bytes 10000000 | tf_op jit(solution)/shard_map/attend/pallas_call | solution.py:136
  189.1 32.5 %own_lin.1.lin_ref = f32[8,1536,384]{2,1,0:T(8,128)} custom-call(bf16[1536,2048]{1,0:T(8,128)(2,1)} %bitcast.139, bf16[2048,2048]{1,0:T(8,128)(2,1)} %wq_ref.7, bf16[2048,1024]{1,0:T(8,128)(2,1)} %wk_ref.7), custom_call_target="tpu_custom_call" | custom-call | flops 19327352832 | bytes 60000000 | tf_op jit(solution)/shard_map/own_lin/pallas_call | solution.py:259
  221.6 19.0 %proj.5 = (bf16[4096,256]{1,0:T(8,128)(2,1)}, bf16[256,4096]{1,0:T(8,128)(2,1)}, bf16[4096,128]{1,0:T(8,128)(2,1)}, bf16[128,4096]{1,0:T(8,128)(2,1)}, bf16[4096...) custom-call(bf16[4096,2048]{1,0:T(8,128)(2,1)} %bitcast.158, ...), custom_call_target="tpu_custom_call" | custom-call | flops 8589934592 | bytes 30000000 | tf_op jit(solution)/shard_map/proj/pallas_call | solution.py:69
  240.6 39.2 %attend.5 = (bf16[4096,256]{1,0:T(8,128)(2,1)}, f32[256,4096]{1,0:T(8,128)}, f32[2,4096]{1,0:T(2,128)}) custom-call(bf16[256,4096]{1,0:T(8,128)(2,1)} %get-tuple-element.167.qt_ref, bf16[4096,128]{1,0:T(8,128)(2,1)} %get-tuple-element.168.k_ref, bf16[128,4096]{1,0:T(8,128)(2,1)} %get-tuple-element.169.vt_ref), custom_call_target="tpu_custom_call" | custom-call | flops 17179869184 | bytes 10000000 | tf_op jit(solution)/shard_map/attend/pallas_call | solution.py:136
  279.9 5.6 constant_dynamic-slice_fusion.32
  290.6 3.0 all-gather.16.cloned.1.call-done
  293.6 19.0 %proj.4 = (bf16[4096,256]{1,0:T(8,128)(2,1)}, bf16[256,4096]{1,0:T(8,128)(2,1)}, bf16[4096,128]{1,0:T(8,128)(2,1)}, bf16[128,4096]{1,0:T(8,128)(2,1)}, bf16[4096...) custom-call(bf16[4096,2048]{1,0:T(8,128)(2,1)} %bitcast.157, ...), custom_call_target="tpu_custom_call" | custom-call | flops 8589934592 | bytes 30000000 | tf_op jit(solution)/shard_map/proj/pallas_call | solution.py:69
  313.9 39.4 %attend.4 = (bf16[4096,256]{1,0:T(8,128)(2,1)}, f32[256,4096]{1,0:T(8,128)}, f32[2,4096]{1,0:T(2,128)}) custom-call(bf16[256,4096]{1,0:T(8,128)(2,1)} %get-tuple-element.152.qt_ref, bf16[4096,128]{1,0:T(8,128)(2,1)} %get-tuple-element.153.k_ref, bf16[128,4096]{1,0:T(8,128)(2,1)} %get-tuple-element.154.vt_ref), custom_call_target="tpu_custom_call" | custom-call | flops 17179869184 | bytes 10000000 | tf_op jit(solution)/shard_map/attend/pallas_call | solution.py:136
  360.3 2.9 collective-permute-done.8
  364.6 3.8 collective-permute-done.9
  370.7 2.1 collective-permute-start.26
  380.7 4.6 collective-permute-done.23
  387.8 43.0 %collective-permute-done.25 = bf16[1536,256]{1,0:T(8,128)(2,1)S(1)} collective-permute-done((bf16[1536,256]{1,0:T(8,128)(2,1)S(1)}, bf16[1536,256]{1,0:T(8,128)(2,1)S(1)}, u32[]{:S(2)}, u32[]{:S(2)}) %collective-permute-start.25) | collective-permute-done | bytes 786464 | tf_op jit(solution)/shard_map/ppermute | solution.py:347
  430.8 2.5 collective-permute-start.30
  443.2 2.4 collective-permute-start.34
  448.1 7.6 collective-permute-done.32
  455.7 2.8 collective-permute-start.16
  460.1 3.1 collective-permute-done.15
  464.0 64.8 %attend_back.3 = (bf16[4096,512]{1,0:T(8,128)(2,1)}, bf16[4096,512]{1,0:T(8,128)(2,1)}, f32[1,128]{1,0:T(1,128)}, f32[1,128]{1,0:T(1,128)}) custom-call(bf16[4096,256]{1,0:T(8,128)(2,1)} %get-tuple-element.173.q_ref, bf16[256,4096]{1,0:T(8,128)(2,1)} %get-tuple-element.146.qt_ref, bf16[3,4096,256]{2,1,0:T(8,128)(2,1)} %constant_dynamic-update-slice_fusion.do_ref, ...), custom_call_target="tpu_custom_call" | custom-call | flops 42949672960 | bytes 20000000 | tf_op jit(solution)/shard_map/attend_back/pallas_call | solution.py:231
  541.3 20.7 %fusion.20 = f32[2048,2048]{1,0:T(8,128)} fusion(bf16[1536,2048]{1,0:T(8,128)(2,1)} %constant_dynamic-update-slice_fusion.24, bf16[1536,2048]{1,0:T(8,128)(2,1)} %bitcast.135), kind=kOutput, calls=%fused_computation.186 | convolution fusion | flops 12884901888 | bytes 29360128 | tf_op jit(solution)/shard_map/dot_general | solution.py:430
  562.1 15.9 %fusion.15 = f32[2048,512]{1,0:T(8,128)} fusion(bf16[4096,512]{1,0:T(8,128)(2,1)} %get-tuple-element.210, bf16[1,4096,2048]{2,1,0:T(8,128)(2,1)} %all-gather.14.cloned.1.call-done), kind=kOutput, calls=%fused_computation.181 | convolution fusion | flops 8589934592 | bytes 25165824 | tf_op jit(solution)/shard_map/dot_general | solution.py:418
  578.0 67.2 %attend_back.4 = (bf16[4096,512]{1,0:T(8,128)(2,1)}, bf16[4096,512]{1,0:T(8,128)(2,1)}, f32[1,128]{1,0:T(1,128)}, f32[1,128]{1,0:T(1,128)}) custom-call(bf16[4096,256]{1,0:T(8,128)(2,1)} %get-tuple-element.212.q_ref, bf16[256,4096]{1,0:T(8,128)(2,1)} %get-tuple-element.167.qt_ref, bf16[3,4096,256]{2,1,0:T(8,128)(2,1)} %constant_dynamic-update-slice_fusion.do_ref, ...), custom_call_target="tpu_custom_call" | custom-call | flops 42949672960 | bytes 20000000 | tf_op jit(solution)/shard_map/attend_back/pallas_call | solution.py:231
  645.2 15.6 %convolution_add_fusion.1 = f32[2048,512]{1,0:T(8,128)} fusion(f32[2048,512]{1,0:T(8,128)} %fusion.15, bf16[4096,512]{1,0:T(8,128)(2,1)} %get-tuple-element.217, bf16[1,4096,2048]{2,1,0:T(8,128)(2,1)} %all-gather.18.cloned.1.call-done), kind=kOutput, calls=%fused_computation.14 | convolution fusion | flops 8590983168 | bytes 29360128 | tf_op jit(solution)/shard_map/dot_general | solution.py:418
  660.8 20.7 %fusion = bf16[1536,2048]{1,0:T(8,128)(2,1)} fusion(bf16[1536,2048]{1,0:T(8,128)(2,1)} %constant_dynamic-update-slice_fusion.24, bf16[2048,2048]{1,0:T(8,128)(2,1)} %param.17, bf16[3,512,2048]{2,1,0:T(8,128)(2,1)} %x_ref.5), kind=kOutput, calls=%fused_computation.1 | convolution fusion | flops 12894339072 | bytes 27262976 | tf_op jit(solution)/shard_map/dot_general | solution.py:22
  682.1 2.8 multiply_sine_fusion.1
  686.6 4.7 constant_dynamic-slice_fusion
  695.2 64.9 %attend_back.5 = (bf16[4096,512]{1,0:T(8,128)(2,1)}, bf16[4096,512]{1,0:T(8,128)(2,1)}, f32[1,128]{1,0:T(1,128)}, f32[1,128]{1,0:T(1,128)}) custom-call(bf16[4096,256]{1,0:T(8,128)(2,1)} %get-tuple-element.220.q_ref, bf16[256,4096]{1,0:T(8,128)(2,1)} %get-tuple-element.152.qt_ref, bf16[3,4096,256]{2,1,0:T(8,128)(2,1)} %constant_dynamic-update-slice_fusion.do_ref, ...), custom_call_target="tpu_custom_call" | custom-call | flops 42949672960 | bytes 20000000 | tf_op jit(solution)/shard_map/attend_back/pallas_call | solution.py:231
  762.5 15.5 %convolution_add_fusion = f32[2048,512]{1,0:T(8,128)} fusion(f32[2048,512]{1,0:T(8,128)} %convolution_add_fusion.1, bf16[4096,512]{1,0:T(8,128)(2,1)} %get-tuple-element.249, bf16[1,4096,2048]{2,1,0:T(8,128)(2,1)} %all-gather.16.cloned.1.call-done), kind=kOutput, calls=%fused_computation.13 | convolution fusion | flops 8590983168 | bytes 29360128 | tf_op jit(solution)/shard_map/dot_general | solution.py:418
  778.0 9.2 collective-permute-done.54
  787.3 18.7 %collective-permute-done.55 = bf16[512,512]{1,0:T(8,128)(2,1)S(1)} collective-permute-done((bf16[512,512]{1,0:T(8,128)(2,1)S(1)}, bf16[512,512]{1,0:T(8,128)(2,1)S(1)}, u32[]{:S(2)}, u32[]{:S(2)}) %collective-permute-start.55) | collective-permute-done | bytes 524320 | tf_op jit(solution)/shard_map/ppermute | solution.py:347
  812.7 30.2 %grad_tokens.3 = (bf16[3,512,2048]{2,1,0:T(8,128)(2,1)}, f32[1,2048]{1,0:T(1,128)}) custom-call(bf16[8,512,512]{2,1,0:T(8,128)(2,1)} %bitcast_dynamic-update-slice_fusion.8.drot_ref, f32[8,1536,384]{2,1,0:T(8,128)} %own_lin.1.lin_ref, bf16[2048,2048]{1,0:T(8,128)(2,1)} %wq_ref.7, bf16[2048,1024]{1,0:T(8,128)(2,1)} %wk_ref.7, bf16[2048,1024]{1,0:T(8,128)(2,1)} %wv_ref.5, ...), custom_call_target="tpu_custom_call" | custom-call | flops 8589934592 | bytes 40000000 | tf_op jit(solution)/shard_map/grad_tokens/pallas_call | solution.py:310
  842.9 4.5 fusion.18
  848.2 4.2 constant_dynamic-slice_fusion.8
  856.5 22.0 %collective-permute-done.43 = bf16[512,512]{1,0:T(8,128)(2,1)S(1)} collective-permute-done((bf16[512,512]{1,0:T(8,128)(2,1)}, bf16[512,512]{1,0:T(8,128)(2,1)S(1)}, u32[]{:S(2)}, u32[]{:S(2)}) %collective-permute-start.43) | collective-permute-done | bytes 524320 | tf_op jit(solution)/shard_map/ppermute | solution.py:347
  878.5 3.8 constant_dynamic-slice_fusion.16
  882.3 18.1 %collective-permute-done.44 = bf16[512,512]{1,0:T(8,128)(2,1)S(1)} collective-permute-done((bf16[512,512]{1,0:T(8,128)(2,1)}, bf16[512,512]{1,0:T(8,128)(2,1)S(1)}, u32[]{:S(2)}, u32[]{:S(2)}) %collective-permute-start.44) | collective-permute-done | bytes 524320 | tf_op jit(solution)/shard_map/ppermute | solution.py:347
  901.5 21.7 %collective-permute-done.46 = bf16[512,512]{1,0:T(8,128)(2,1)S(1)} collective-permute-done((bf16[512,512]{1,0:T(8,128)(2,1)}, bf16[512,512]{1,0:T(8,128)(2,1)S(1)}, u32[]{:S(2)}, u32[]{:S(2)}) %collective-permute-start.46) | collective-permute-done | bytes 524320 | tf_op jit(solution)/shard_map/ppermute | solution.py:347
  933.6 7.0 collective-permute-done.36
  940.7 30.1 %grad_tokens.4 = (bf16[3,512,2048]{2,1,0:T(8,128)(2,1)}, f32[1,2048]{1,0:T(1,128)}) custom-call(bf16[8,512,512]{2,1,0:T(8,128)(2,1)} %bitcast_dynamic-update-slice_fusion.16.drot_ref, f32[8,1536,384]{2,1,0:T(8,128)} %own_lin.1.lin_ref, bf16[2048,2048]{1,0:T(8,128)(2,1)} %wq_ref.7, bf16[2048,1024]{1,0:T(8,128)(2,1)} %wk_ref.7, ...), custom_call_target="tpu_custom_call", output_to_operand_aliasing={{0}: (12, {})} | custom-call | flops 8589934592 | bytes 40000000 | tf_op jit(solution)/shard_map/grad_tokens/pallas_call | solution.py:310
  970.8 9.7 collective-permute-done.39
  980.5 4.9 collective-permute-done.40
  985.4 20.7 %collective-permute-done.41 = bf16[512,512]{1,0:T(8,128)(2,1)S(1)} collective-permute-done((bf16[512,512]{1,0:T(8,128)(2,1)}, bf16[512,512]{1,0:T(8,128)(2,1)S(1)}, u32[]{:S(2)}, u32[]{:S(2)}) %collective-permute-start.41) | collective-permute-done | bytes 524320 | tf_op jit(solution)/shard_map/ppermute | solution.py:347
  1018.0 30.4 %grad_tokens.5 = (bf16[3,512,2048]{2,1,0:T(8,128)(2,1)}, f32[1,2048]{1,0:T(1,128)}) custom-call(bf16[8,512,512]{2,1,0:T(8,128)(2,1)} %bitcast_dynamic-update-slice_fusion.drot_ref, f32[8,1536,384]{2,1,0:T(8,128)} %own_lin.1.lin_ref, bf16[2048,2048]{1,0:T(8,128)(2,1)} %wq_ref.7, bf16[2048,1024]{1,0:T(8,128)(2,1)} %wk_ref.7, ...), custom_call_target="tpu_custom_call", output_to_operand_aliasing={{0}: (12, {})} | custom-call | flops 8589934592 | bytes 40000000 | tf_op jit(solution)/shard_map/grad_tokens/pallas_call | solution.py:310
  1051.5 3.0 collective-permute-done.57
  1054.5 2.2 collective-permute-start.58
  1059.5 6.5 slice_bitcast_fusion
  1066.0 4.6 copy.29
  1070.6 4.6 copy.30
  1075.2 30.3 %all-gather.20.cloned.1.call-done = f32[16384,256]{1,0:T(8,128)} async-done(((f32[2048,256]{1,0:T(8,128)}), f32[16384,256]{1,0:T(8,128)}) %all-gather.20.cloned.1.call-update) | async-done | bytes 16777232 | tf_op jit(solution)/shard_map/all_gather | solution.py:446
  1105.5 13.8 %copy.24 = f32[8,256,8,256]{3,2,0,1:T(8,128)} copy(f32[8,256,8,256]{3,2,1,0:T(8,128)} %bitcast.143) | data formatting | bytes 33554432 | tf_op jit(solution)/shard_map/reshape | solution.py:446
  1122.0 6.2 copy.98
  (273 shorter events, 120.6 us)
Async XLA Ops:
  7.2 113.6 %all-gather.14.cloned.1.call-start = ((), (), s32[]{:S(2)}) async-start(), calls=%async_computation.3 | async-start | bytes 18874368 | tf_op jit(solution)/shard_map/all_gather | solution.py:367
  7.2 17.7 %collective-permute-start = (s32[3,512]{1,0:T(4,128)}, s32[3,512]{1,0:T(4,128)S(1)}, u32[]{:S(2)}, u32[]{:S(2)}) collective-permute-start(s32[3,512]{1,0:T(4,128)} %param.12), channel_id=1, source_target_pairs={{0,1},{1,0},{2,3},{3,2},{4,5},{5,4},{6,7},{7,6}} | collective-permute-start | bytes 18440 | tf_op jit(solution)/shard_map/ppermute | solution.py:347
  8.1 19.4 %collective-permute-start.1 = (s32[3,512]{1,0:T(4,128)}, s32[3,512]{1,0:T(4,128)S(1)}, u32[]{:S(2)}, u32[]{:S(2)}) collective-permute-start(s32[3,512]{1,0:T(4,128)} %param.12), channel_id=1, source_target_pairs={{0,2},{1,3},{2,0},{3,1},{4,6},{5,7},{6,4},{7,5}} | collective-permute-start | bytes 18440 | tf_op jit(solution)/shard_map/ppermute | solution.py:347
  10.6 17.0 %collective-permute-start.2 = (s32[3,512]{1,0:T(4,128)}, s32[3,512]{1,0:T(4,128)S(1)}, u32[]{:S(2)}, u32[]{:S(2)}) collective-permute-start(s32[3,512]{1,0:T(4,128)} %param.12), channel_id=1, source_target_pairs={{0,3},{1,2},{2,1},{3,0},{4,7},{5,6},{6,5},{7,4}} | collective-permute-start | bytes 18440 | tf_op jit(solution)/shard_map/ppermute | solution.py:347
  10.7 17.0 %collective-permute-start.3 = (s32[3,512]{1,0:T(4,128)}, s32[3,512]{1,0:T(4,128)S(1)}, u32[]{:S(2)}, u32[]{:S(2)}) collective-permute-start(s32[3,512]{1,0:T(4,128)} %param.12), channel_id=1, source_target_pairs={{0,4},{1,5},{2,6},{3,7},{4,0},{5,1},{6,2},{7,3}} | collective-permute-start | bytes 18440 | tf_op jit(solution)/shard_map/ppermute | solution.py:347
  12.4 15.2 %collective-permute-start.4 = (s32[3,512]{1,0:T(4,128)}, s32[3,512]{1,0:T(4,128)S(1)}, u32[]{:S(2)}, u32[]{:S(2)}) collective-permute-start(s32[3,512]{1,0:T(4,128)} %param.12), channel_id=1, source_target_pairs={{0,5},{1,4},{2,7},{3,6},{4,1},{5,0},{6,3},{7,2}} | collective-permute-start | bytes 18440 | tf_op jit(solution)/shard_map/ppermute | solution.py:347
  24.9 4.6 collective-permute-start.5
  27.5 4.0 collective-permute-start.6
  37.3 184.3 %all-gather.18.cloned.1.call-start = ((), (), s32[]{:S(2)}) async-start(), calls=%async_computation.5 | async-start | bytes 18874368 | tf_op jit(solution)/shard_map/all_gather | solution.py:367
  38.1 255.5 %all-gather.16.cloned.1.call-start = ((), (), s32[]{:S(2)}) async-start(), calls=%async_computation.4 | async-start | bytes 18874368 | tf_op jit(solution)/shard_map/all_gather | solution.py:367
  38.8 642.6 %reduce-scatter.2.cloned.1.call-start = ((), (), s32[]{:S(2)}) async-start(), calls=%async_computation.1 | async-start | bytes 18874368 | tf_op jit(solution)/shard_map/reduce_scatter | solution.py:431
  285.4 85.2 %collective-permute-start.21 = (bf16[1536,256]{1,0:T(8,128)(2,1)}, bf16[1536,256]{1,0:T(8,128)(2,1)}, u32[]{:S(2)}, u32[]{:S(2)}) collective-permute-start(bf16[1536,256]{1,0:T(8,128)(2,1)} %get-tuple-element.283), channel_id=1, source_target_pairs={{0,1},{1,0},{2,3},{3,2},{4,5},{5,4},{6,7},{7,6}} | collective-permute-start | bytes 2359304 | tf_op jit(solution)/shard_map/ppermute | solution.py:347
  285.7 87.1 %collective-permute-start.22 = (bf16[1536,256]{1,0:T(8,128)(2,1)}, bf16[1536,256]{1,0:T(8,128)(2,1)}, u32[]{:S(2)}, u32[]{:S(2)}) collective-permute-start(bf16[1536,256]{1,0:T(8,128)(2,1)} %get-tuple-element.282), channel_id=1, source_target_pairs={{0,2},{1,3},{2,0},{3,1},{4,6},{5,7},{6,4},{7,5}} | collective-permute-start | bytes 2359304 | tf_op jit(solution)/shard_map/ppermute | solution.py:347
  288.4 24.2 %collective-permute-start.10 = (bf16[512,256]{1,0:T(8,128)(2,1)}, bf16[512,256]{1,0:T(8,128)(2,1)S(1)}, u32[]{:S(2)}, u32[]{:S(2)}) collective-permute-start(bf16[512,256]{1,0:T(8,128)(2,1)} %get-tuple-element.339), channel_id=1, source_target_pairs={{0,4},{1,5},{2,6},{3,7},{4,0},{5,1},{6,2},{7,3}} | collective-permute-start | bytes 786440 | tf_op jit(solution)/shard_map/ppermute | solution.py:347
  289.0 64.6 %collective-permute-start.11 = (bf16[512,256]{1,0:T(8,128)(2,1)}, bf16[512,256]{1,0:T(8,128)(2,1)}, u32[]{:S(2)}, u32[]{:S(2)}) collective-permute-start(bf16[512,256]{1,0:T(8,128)(2,1)} %get-tuple-element.338), channel_id=1, source_target_pairs={{0,5},{1,4},{2,7},{3,6},{4,1},{5,0},{6,3},{7,2}} | collective-permute-start | bytes 786440 | tf_op jit(solution)/shard_map/ppermute | solution.py:347
  289.7 64.1 %collective-permute-start.12 = (bf16[512,256]{1,0:T(8,128)(2,1)}, bf16[512,256]{1,0:T(8,128)(2,1)}, u32[]{:S(2)}, u32[]{:S(2)}) collective-permute-start(bf16[512,256]{1,0:T(8,128)(2,1)} %get-tuple-element.337), channel_id=1, source_target_pairs={{0,6},{1,7},{2,4},{3,5},{4,2},{5,3},{6,0},{7,1}} | collective-permute-start | bytes 786440 | tf_op jit(solution)/shard_map/ppermute | solution.py:347
  312.6 43.2 %collective-permute-start.13 = (bf16[512,256]{1,0:T(8,128)(2,1)}, bf16[512,256]{1,0:T(8,128)(2,1)}, u32[]{:S(2)}, u32[]{:S(2)}) collective-permute-start(bf16[512,256]{1,0:T(8,128)(2,1)} %get-tuple-element.336), channel_id=1, source_target_pairs={{0,7},{1,6},{2,5},{3,4},{4,3},{5,2},{6,1},{7,0}} | collective-permute-start | bytes 786440 | tf_op jit(solution)/shard_map/ppermute | solution.py:347
  353.5 5.1 collective-permute-start.7
  353.8 9.4 collective-permute-start.8
  355.9 12.5 %collective-permute-start.9 = (bf16[512,256]{1,0:T(8,128)(2,1)S(1)}, bf16[512,256]{1,0:T(8,128)(2,1)S(1)}, u32[]{:S(2)}, u32[]{:S(2)}) collective-permute-start(bf16[512,256]{1,0:T(8,128)(2,1)S(1)} %get-tuple-element.340), channel_id=1, source_target_pairs={{0,3},{1,2},{2,1},{3,0},{4,7},{5,6},{6,5},{7,4}} | collective-permute-start | bytes 786440 | tf_op jit(solution)/shard_map/ppermute | solution.py:347
  358.6 26.6 %collective-permute-start.23 = (bf16[1536,256]{1,0:T(8,128)(2,1)S(1)}, bf16[1536,256]{1,0:T(8,128)(2,1)S(1)}, u32[]{:S(2)}, u32[]{:S(2)}) collective-permute-start(bf16[1536,256]{1,0:T(8,128)(2,1)S(1)} %copy-done.7), channel_id=1, source_target_pairs={{0,3},{1,2},{2,1},{3,0},{4,7},{5,6},{6,5},{7,4}} | collective-permute-start | bytes 2359304 | tf_op jit(solution)/shard_map/ppermute | solution.py:347
  363.2 22.6 %collective-permute-start.24 = (bf16[1536,256]{1,0:T(8,128)(2,1)S(1)}, bf16[1536,256]{1,0:T(8,128)(2,1)S(1)}, u32[]{:S(2)}, u32[]{:S(2)}) collective-permute-start(bf16[1536,256]{1,0:T(8,128)(2,1)S(1)} %copy-done.6), channel_id=1, source_target_pairs={{0,4},{1,5},{2,6},{3,7},{4,0},{5,1},{6,2},{7,3}} | collective-permute-start | bytes 2359304 | tf_op jit(solution)/shard_map/ppermute | solution.py:347
  368.4 62.5 %collective-permute-start.25 = (bf16[1536,256]{1,0:T(8,128)(2,1)S(1)}, bf16[1536,256]{1,0:T(8,128)(2,1)S(1)}, u32[]{:S(2)}, u32[]{:S(2)}) collective-permute-start(bf16[1536,256]{1,0:T(8,128)(2,1)S(1)} %copy-done.5), channel_id=1, source_target_pairs={{0,5},{1,4},{2,7},{3,6},{4,1},{5,0},{6,3},{7,2}} | collective-permute-start | bytes 2359304 | tf_op jit(solution)/shard_map/ppermute | solution.py:347
  370.7 62.7 %collective-permute-start.26 = (bf16[1536,256]{1,0:T(8,128)(2,1)S(1)}, bf16[1536,256]{1,0:T(8,128)(2,1)S(1)}, u32[]{:S(2)}, u32[]{:S(2)}) collective-permute-start(bf16[1536,256]{1,0:T(8,128)(2,1)S(1)} %copy-done.4), channel_id=1, source_target_pairs={{0,6},{1,7},{2,4},{3,5},{4,2},{5,3},{6,0},{7,1}} | collective-permute-start | bytes 2359304 | tf_op jit(solution)/shard_map/ppermute | solution.py:347
  372.8 60.9 %collective-permute-start.27 = (bf16[1536,256]{1,0:T(8,128)(2,1)S(1)}, bf16[1536,256]{1,0:T(8,128)(2,1)S(1)}, u32[]{:S(2)}, u32[]{:S(2)}) collective-permute-start(bf16[1536,256]{1,0:T(8,128)(2,1)S(1)} %copy-done.3), channel_id=1, source_target_pairs={{0,7},{1,6},{2,5},{3,4},{4,3},{5,2},{6,1},{7,0}} | collective-permute-start | bytes 2359304 | tf_op jit(solution)/shard_map/ppermute | solution.py:347
  385.2 56.3 %collective-permute-start.28 = (bf16[512,256]{1,0:T(8,128)(2,1)S(1)}, bf16[512,256]{1,0:T(8,128)(2,1)S(1)}, u32[]{:S(2)}, u32[]{:S(2)}) collective-permute-start(bf16[512,256]{1,0:T(8,128)(2,1)S(1)} %get-tuple-element.326), channel_id=1, source_target_pairs={{0,1},{1,0},{2,3},{3,2},{4,5},{5,4},{6,7},{7,6}} | collective-permute-start | bytes 786440 | tf_op jit(solution)/shard_map/ppermute | solution.py:347
  385.8 57.4 %collective-permute-start.29 = (bf16[512,256]{1,0:T(8,128)(2,1)S(1)}, bf16[512,256]{1,0:T(8,128)(2,1)S(1)}, u32[]{:S(2)}, u32[]{:S(2)}) collective-permute-start(bf16[512,256]{1,0:T(8,128)(2,1)S(1)} %get-tuple-element.325), channel_id=1, source_target_pairs={{0,2},{1,3},{2,0},{3,1},{4,6},{5,7},{6,4},{7,5}} | collective-permute-start | bytes 786440 | tf_op jit(solution)/shard_map/ppermute | solution.py:347
  430.8 14.8 %collective-permute-start.30 = (bf16[512,256]{1,0:T(8,128)(2,1)S(1)}, bf16[512,256]{1,0:T(8,128)(2,1)S(1)}, u32[]{:S(2)}, u32[]{:S(2)}) collective-permute-start(bf16[512,256]{1,0:T(8,128)(2,1)S(1)} %get-tuple-element.324), channel_id=1, source_target_pairs={{0,3},{1,2},{2,1},{3,0},{4,7},{5,6},{6,5},{7,4}} | collective-permute-start | bytes 786440 | tf_op jit(solution)/shard_map/ppermute | solution.py:347
  433.4 12.3 %collective-permute-start.31 = (bf16[512,256]{1,0:T(8,128)(2,1)S(1)}, bf16[512,256]{1,0:T(8,128)(2,1)S(1)}, u32[]{:S(2)}, u32[]{:S(2)}) collective-permute-start(bf16[512,256]{1,0:T(8,128)(2,1)S(1)} %get-tuple-element.323), channel_id=1, source_target_pairs={{0,4},{1,5},{2,6},{3,7},{4,0},{5,1},{6,2},{7,3}} | collective-permute-start | bytes 786440 | tf_op jit(solution)/shard_map/ppermute | solution.py:347
  433.6 22.1 %collective-permute-start.32 = (bf16[512,256]{1,0:T(8,128)(2,1)S(1)}, bf16[512,256]{1,0:T(8,128)(2,1)S(1)}, u32[]{:S(2)}, u32[]{:S(2)}) collective-permute-start(bf16[512,256]{1,0:T(8,128)(2,1)S(1)} %get-tuple-element.322), channel_id=1, source_target_pairs={{0,5},{1,4},{2,7},{3,6},{4,1},{5,0},{6,3},{7,2}} | collective-permute-start | bytes 786440 | tf_op jit(solution)/shard_map/ppermute | solution.py:347
  441.5 17.0 %collective-permute-start.33 = (bf16[512,256]{1,0:T(8,128)(2,1)S(1)}, bf16[512,256]{1,0:T(8,128)(2,1)S(1)}, u32[]{:S(2)}, u32[]{:S(2)}) collective-permute-start(bf16[512,256]{1,0:T(8,128)(2,1)S(1)} %get-tuple-element.321), channel_id=1, source_target_pairs={{0,6},{1,7},{2,4},{3,5},{4,2},{5,3},{6,0},{7,1}} | collective-permute-start | bytes 786440 | tf_op jit(solution)/shard_map/ppermute | solution.py:347
  443.2 15.3 %collective-permute-start.34 = (bf16[512,256]{1,0:T(8,128)(2,1)S(1)}, bf16[512,256]{1,0:T(8,128)(2,1)S(1)}, u32[]{:S(2)}, u32[]{:S(2)}) collective-permute-start(bf16[512,256]{1,0:T(8,128)(2,1)S(1)} %get-tuple-element.320), channel_id=1, source_target_pairs={{0,7},{1,6},{2,5},{3,4},{4,3},{5,2},{6,1},{7,0}} | collective-permute-start | bytes 786440 | tf_op jit(solution)/shard_map/ppermute | solution.py:347
  445.6 13.0 %collective-permute-start.14 = (bf16[512,256]{1,0:T(8,128)(2,1)S(1)}, bf16[512,256]{1,0:T(8,128)(2,1)S(1)}, u32[]{:S(2)}, u32[]{:S(2)}) collective-permute-start(bf16[512,256]{1,0:T(8,128)(2,1)S(1)} %get-tuple-element.334), channel_id=1, source_target_pairs={{0,1},{1,0},{2,3},{3,2},{4,5},{5,4},{6,7},{7,6}} | collective-permute-start | bytes 786440 | tf_op jit(solution)/shard_map/ppermute | solution.py:347
  445.6 17.5 %collective-permute-start.15 = (bf16[512,256]{1,0:T(8,128)(2,1)S(1)}, bf16[512,256]{1,0:T(8,128)(2,1)S(1)}, u32[]{:S(2)}, u32[]{:S(2)}) collective-permute-start(bf16[512,256]{1,0:T(8,128)(2,1)S(1)} %get-tuple-element.333), channel_id=1, source_target_pairs={{0,2},{1,3},{2,0},{3,1},{4,6},{5,7},{6,4},{7,5}} | collective-permute-start | bytes 786440 | tf_op jit(solution)/shard_map/ppermute | solution.py:347
  455.7 73.1 %collective-permute-start.16 = (bf16[512,256]{1,0:T(8,128)(2,1)}, bf16[512,256]{1,0:T(8,128)(2,1)S(1)}, u32[]{:S(2)}, u32[]{:S(2)}) collective-permute-start(bf16[512,256]{1,0:T(8,128)(2,1)} %get-tuple-element.332), channel_id=1, source_target_pairs={{0,3},{1,2},{2,1},{3,0},{4,7},{5,6},{6,5},{7,4}} | collective-permute-start | bytes 786440 | tf_op jit(solution)/shard_map/ppermute | solution.py:347
  458.5 70.3 %collective-permute-start.17 = (bf16[512,256]{1,0:T(8,128)(2,1)}, bf16[512,256]{1,0:T(8,128)(2,1)S(1)}, u32[]{:S(2)}, u32[]{:S(2)}) collective-permute-start(bf16[512,256]{1,0:T(8,128)(2,1)} %get-tuple-element.331), channel_id=1, source_target_pairs={{0,4},{1,5},{2,6},{3,7},{4,0},{5,1},{6,2},{7,3}} | collective-permute-start | bytes 786440 | tf_op jit(solution)/shard_map/ppermute | solution.py:347
  458.6 70.3 %collective-permute-start.18 = (bf16[512,256]{1,0:T(8,128)(2,1)}, bf16[512,256]{1,0:T(8,128)(2,1)S(1)}, u32[]{:S(2)}, u32[]{:S(2)}) collective-permute-start(bf16[512,256]{1,0:T(8,128)(2,1)} %get-tuple-element.330), channel_id=1, source_target_pairs={{0,5},{1,4},{2,7},{3,6},{4,1},{5,0},{6,3},{7,2}} | collective-permute-start | bytes 786440 | tf_op jit(solution)/shard_map/ppermute | solution.py:347
  458.6 70.3 %collective-permute-start.19 = (bf16[512,256]{1,0:T(8,128)(2,1)}, bf16[512,256]{1,0:T(8,128)(2,1)S(1)}, u32[]{:S(2)}, u32[]{:S(2)}) collective-permute-start(bf16[512,256]{1,0:T(8,128)(2,1)} %get-tuple-element.329), channel_id=1, source_target_pairs={{0,6},{1,7},{2,4},{3,5},{4,2},{5,3},{6,0},{7,1}} | collective-permute-start | bytes 786440 | tf_op jit(solution)/shard_map/ppermute | solution.py:347
  463.1 65.7 %collective-permute-start.20 = (bf16[512,256]{1,0:T(8,128)(2,1)}, bf16[512,256]{1,0:T(8,128)(2,1)}, u32[]{:S(2)}, u32[]{:S(2)}) collective-permute-start(bf16[512,256]{1,0:T(8,128)(2,1)} %get-tuple-element.328), channel_id=1, source_target_pairs={{0,7},{1,6},{2,5},{3,4},{4,3},{5,2},{6,1},{7,0}} | collective-permute-start | bytes 786440 | tf_op jit(solution)/shard_map/ppermute | solution.py:347
  562.0 280.8 %all-gather.12.cloned.1.call-start = ((), (), s32[]{:S(2)}) async-start(), calls=%async_computation.2 | async-start | bytes 18874368 | tf_op jit(solution)/shard_map/all_gather | solution.py:435
  681.5 378.0 %all-gather.22.cloned.1.call-start = ((), (), s32[]{:S(2)}) async-start(), calls=%async_computation.7 | async-start | bytes 18874368 | tf_op jit(solution)/shard_map/all_gather | solution.py:450
  691.2 68.9 %collective-permute-start.49 = (bf16[512,512]{1,0:T(8,128)(2,1)}, bf16[512,512]{1,0:T(8,128)(2,1)S(1)}, u32[]{:S(2)}, u32[]{:S(2)}) collective-permute-start(bf16[512,512]{1,0:T(8,128)(2,1)} %get-tuple-element.302), channel_id=1, source_target_pairs={{0,1},{1,0},{2,3},{3,2},{4,5},{5,4},{6,7},{7,6}} | collective-permute-start | bytes 1572872 | tf_op jit(solution)/shard_map/ppermute | solution.py:347
  691.7 70.4 %collective-permute-start.50 = (bf16[512,512]{1,0:T(8,128)(2,1)}, bf16[512,512]{1,0:T(8,128)(2,1)S(1)}, u32[]{:S(2)}, u32[]{:S(2)}) collective-permute-start(bf16[512,512]{1,0:T(8,128)(2,1)} %get-tuple-element.301), channel_id=1, source_target_pairs={{0,2},{1,3},{2,0},{3,1},{4,6},{5,7},{6,4},{7,5}} | collective-permute-start | bytes 1572872 | tf_op jit(solution)/shard_map/ppermute | solution.py:347
  692.7 85.3 %collective-permute-start.51 = (bf16[512,512]{1,0:T(8,128)(2,1)}, bf16[512,512]{1,0:T(8,128)(2,1)S(1)}, u32[]{:S(2)}, u32[]{:S(2)}) collective-permute-start(bf16[512,512]{1,0:T(8,128)(2,1)} %get-tuple-element.300), channel_id=1, source_target_pairs={{0,3},{1,2},{2,1},{3,0},{4,7},{5,6},{6,5},{7,4}} | collective-permute-start | bytes 1572872 | tf_op jit(solution)/shard_map/ppermute | solution.py:347
  693.1 84.9 %collective-permute-start.52 = (bf16[512,512]{1,0:T(8,128)(2,1)}, bf16[512,512]{1,0:T(8,128)(2,1)S(1)}, u32[]{:S(2)}, u32[]{:S(2)}) collective-permute-start(bf16[512,512]{1,0:T(8,128)(2,1)} %get-tuple-element.299), channel_id=1, source_target_pairs={{0,4},{1,5},{2,6},{3,7},{4,0},{5,1},{6,2},{7,3}} | collective-permute-start | bytes 1572872 | tf_op jit(solution)/shard_map/ppermute | solution.py:347
  694.2 83.8 %collective-permute-start.53 = (bf16[512,512]{1,0:T(8,128)(2,1)}, bf16[512,512]{1,0:T(8,128)(2,1)S(1)}, u32[]{:S(2)}, u32[]{:S(2)}) collective-permute-start(bf16[512,512]{1,0:T(8,128)(2,1)} %get-tuple-element.298), channel_id=1, source_target_pairs={{0,5},{1,4},{2,7},{3,6},{4,1},{5,0},{6,3},{7,2}} | collective-permute-start | bytes 1572872 | tf_op jit(solution)/shard_map/ppermute | solution.py:347
  760.1 27.2 %collective-permute-start.54 = (bf16[512,512]{1,0:T(8,128)(2,1)}, bf16[512,512]{1,0:T(8,128)(2,1)S(1)}, u32[]{:S(2)}, u32[]{:S(2)}) collective-permute-start(bf16[512,512]{1,0:T(8,128)(2,1)} %get-tuple-element.297), channel_id=1, source_target_pairs={{0,6},{1,7},{2,4},{3,5},{4,2},{5,3},{6,0},{7,1}} | collective-permute-start | bytes 1572872 | tf_op jit(solution)/shard_map/ppermute | solution.py:347
  762.1 43.8 %collective-permute-start.55 = (bf16[512,512]{1,0:T(8,128)(2,1)S(1)}, bf16[512,512]{1,0:T(8,128)(2,1)S(1)}, u32[]{:S(2)}, u32[]{:S(2)}) collective-permute-start(bf16[512,512]{1,0:T(8,128)(2,1)S(1)} %get-tuple-element.296), channel_id=1, source_target_pairs={{0,7},{1,6},{2,5},{3,4},{4,3},{5,2},{6,1},{7,0}} | collective-permute-start | bytes 1572872 | tf_op jit(solution)/shard_map/ppermute | solution.py:347
  847.4 258.0 %all-gather.20.cloned.1.call-start = ((), (), s32[]{:S(2)}) async-start(), calls=%async_computation.6 | async-start | bytes 18874368 | tf_op jit(solution)/shard_map/all_gather | solution.py:446
  852.5 26.0 %collective-permute-start.43 = (bf16[512,512]{1,0:T(8,128)(2,1)}, bf16[512,512]{1,0:T(8,128)(2,1)S(1)}, u32[]{:S(2)}, u32[]{:S(2)}) collective-permute-start(bf16[512,512]{1,0:T(8,128)(2,1)} %get-tuple-element.309), channel_id=1, source_target_pairs={{0,2},{1,3},{2,0},{3,1},{4,6},{5,7},{6,4},{7,5}} | collective-permute-start | bytes 1572872 | tf_op jit(solution)/shard_map/ppermute | solution.py:347
  853.2 47.3 %collective-permute-start.44 = (bf16[512,512]{1,0:T(8,128)(2,1)}, bf16[512,512]{1,0:T(8,128)(2,1)S(1)}, u32[]{:S(2)}, u32[]{:S(2)}) collective-permute-start(bf16[512,512]{1,0:T(8,128)(2,1)} %get-tuple-element.308), channel_id=1, source_target_pairs={{0,3},{1,2},{2,1},{3,0},{4,7},{5,6},{6,5},{7,4}} | collective-permute-start | bytes 1572872 | tf_op jit(solution)/shard_map/ppermute | solution.py:347
  854.4 46.6 %collective-permute-start.45 = (bf16[512,512]{1,0:T(8,128)(2,1)}, bf16[512,512]{1,0:T(8,128)(2,1)S(1)}, u32[]{:S(2)}, u32[]{:S(2)}) collective-permute-start(bf16[512,512]{1,0:T(8,128)(2,1)} %get-tuple-element.307), channel_id=1, source_target_pairs={{0,4},{1,5},{2,6},{3,7},{4,0},{5,1},{6,2},{7,3}} | collective-permute-start | bytes 1572872 | tf_op jit(solution)/shard_map/ppermute | solution.py:347
  854.9 68.3 %collective-permute-start.46 = (bf16[512,512]{1,0:T(8,128)(2,1)}, bf16[512,512]{1,0:T(8,128)(2,1)S(1)}, u32[]{:S(2)}, u32[]{:S(2)}) collective-permute-start(bf16[512,512]{1,0:T(8,128)(2,1)} %get-tuple-element.306), channel_id=1, source_target_pairs={{0,5},{1,4},{2,7},{3,6},{4,1},{5,0},{6,3},{7,2}} | collective-permute-start | bytes 1572872 | tf_op jit(solution)/shard_map/ppermute | solution.py:347
  856.1 68.9 %collective-permute-start.47 = (bf16[512,512]{1,0:T(8,128)(2,1)}, bf16[512,512]{1,0:T(8,128)(2,1)S(1)}, u32[]{:S(2)}, u32[]{:S(2)}) collective-permute-start(bf16[512,512]{1,0:T(8,128)(2,1)} %get-tuple-element.305), channel_id=1, source_target_pairs={{0,6},{1,7},{2,4},{3,5},{4,2},{5,3},{6,0},{7,1}} | collective-permute-start | bytes 1572872 | tf_op jit(solution)/shard_map/ppermute | solution.py:347
  878.5 47.1 %collective-permute-start.48 = (bf16[512,512]{1,0:T(8,128)(2,1)}, bf16[512,512]{1,0:T(8,128)(2,1)S(1)}, u32[]{:S(2)}, u32[]{:S(2)}) collective-permute-start(bf16[512,512]{1,0:T(8,128)(2,1)} %get-tuple-element.304), channel_id=1, source_target_pairs={{0,7},{1,6},{2,5},{3,4},{4,3},{5,2},{6,1},{7,0}} | collective-permute-start | bytes 1572872 | tf_op jit(solution)/shard_map/ppermute | solution.py:347
  900.5 32.6 %collective-permute-start.35 = (bf16[512,512]{1,0:T(8,128)(2,1)S(1)}, bf16[512,512]{1,0:T(8,128)(2,1)}, u32[]{:S(2)}, u32[]{:S(2)}) collective-permute-start(bf16[512,512]{1,0:T(8,128)(2,1)S(1)} %get-tuple-element.318), channel_id=1, source_target_pairs={{0,1},{1,0},{2,3},{3,2},{4,5},{5,4},{6,7},{7,6}} | collective-permute-start | bytes 1572872 | tf_op jit(solution)/shard_map/ppermute | solution.py:347
  901.1 39.6 %collective-permute-start.36 = (bf16[512,512]{1,0:T(8,128)(2,1)S(1)}, bf16[512,512]{1,0:T(8,128)(2,1)}, u32[]{:S(2)}, u32[]{:S(2)}) collective-permute-start(bf16[512,512]{1,0:T(8,128)(2,1)S(1)} %get-tuple-element.317), channel_id=1, source_target_pairs={{0,2},{1,3},{2,0},{3,1},{4,6},{5,7},{6,4},{7,5}} | collective-permute-start | bytes 1572872 | tf_op jit(solution)/shard_map/ppermute | solution.py:347
  923.2 47.6 %collective-permute-start.37 = (bf16[512,512]{1,0:T(8,128)(2,1)}, bf16[512,512]{1,0:T(8,128)(2,1)}, u32[]{:S(2)}, u32[]{:S(2)}) collective-permute-start(bf16[512,512]{1,0:T(8,128)(2,1)} %get-tuple-element.316), channel_id=1, source_target_pairs={{0,3},{1,2},{2,1},{3,0},{4,7},{5,6},{6,5},{7,4}} | collective-permute-start | bytes 1572872 | tf_op jit(solution)/shard_map/ppermute | solution.py:347
  925.0 45.9 %collective-permute-start.38 = (bf16[512,512]{1,0:T(8,128)(2,1)}, bf16[512,512]{1,0:T(8,128)(2,1)}, u32[]{:S(2)}, u32[]{:S(2)}) collective-permute-start(bf16[512,512]{1,0:T(8,128)(2,1)} %get-tuple-element.315), channel_id=1, source_target_pairs={{0,4},{1,5},{2,6},{3,7},{4,0},{5,1},{6,2},{7,3}} | collective-permute-start | bytes 1572872 | tf_op jit(solution)/shard_map/ppermute | solution.py:347
  925.5 55.0 %collective-permute-start.39 = (bf16[512,512]{1,0:T(8,128)(2,1)}, bf16[512,512]{1,0:T(8,128)(2,1)}, u32[]{:S(2)}, u32[]{:S(2)}) collective-permute-start(bf16[512,512]{1,0:T(8,128)(2,1)} %get-tuple-element.314), channel_id=1, source_target_pairs={{0,5},{1,4},{2,7},{3,6},{4,1},{5,0},{6,3},{7,2}} | collective-permute-start | bytes 1572872 | tf_op jit(solution)/shard_map/ppermute | solution.py:347
  933.1 52.3 %collective-permute-start.40 = (bf16[512,512]{1,0:T(8,128)(2,1)}, bf16[512,512]{1,0:T(8,128)(2,1)S(1)}, u32[]{:S(2)}, u32[]{:S(2)}) collective-permute-start(bf16[512,512]{1,0:T(8,128)(2,1)} %get-tuple-element.313), channel_id=1, source_target_pairs={{0,6},{1,7},{2,4},{3,5},{4,2},{5,3},{6,0},{7,1}} | collective-permute-start | bytes 1572872 | tf_op jit(solution)/shard_map/ppermute | solution.py:347
  940.7 65.4 %collective-permute-start.41 = (bf16[512,512]{1,0:T(8,128)(2,1)}, bf16[512,512]{1,0:T(8,128)(2,1)S(1)}, u32[]{:S(2)}, u32[]{:S(2)}) collective-permute-start(bf16[512,512]{1,0:T(8,128)(2,1)} %get-tuple-element.312), channel_id=1, source_target_pairs={{0,7},{1,6},{2,5},{3,4},{4,3},{5,2},{6,1},{7,0}} | collective-permute-start | bytes 1572872 | tf_op jit(solution)/shard_map/ppermute | solution.py:347
  1050.8 3.7 collective-permute-start.57
  1054.5 3.9 collective-permute-start.58
  (36 other events, 527.7 us)
Sparse Core Ops, SparseCore 0:
  37.4 83.2 all-gather.13
  122.6 84.1 all-gather.17
  208.6 84.9 all-gather.15
  562.2 108.1 reduce-scatter.1
  681.6 122.2 all-gather.11
  847.6 172.7 all-gather.21
  1022.2 83.2 all-gather.19
where the time goes:
time: 1140 us
  Pallas kernels  496 us (44%)
  waiting for transfers between devices  271 us (24%)
  local copies, waits for them, and re-layouts  143 us (13%)
  matrix products  106 us (9%)
  starting transfers between devices  56.6 us (5%)
  other arithmetic  48.4 us (4%)
  between operations  15.5 us (1%)
    ppermute x59, waiting for transfers between devices, swap(): return lax.ppermute(x, SEQ_AXIS, [(d, d ^ dist) for d in range(n_dev)])  206 us
    pallas_call x3, Pallas kernels, attend_back(): pl.pallas_call(bwd_kernel, grid=(toks // BLK,), in_specs=[whole(q), whole...  197 us
    pallas_call x3, Pallas kernels, attend(): pl.pallas_call(fwd_kernel, grid=(toks // BLK,), in_specs=[pl.BlockSpec((2...  118 us
    pallas_call x3, Pallas kernels, grad_tokens(): pl.pallas_call(gradx_kernel, grid=(groups,), in_specs=[pl.BlockSpec((1, t...  90.7 us
    pallas_call x3, Pallas kernels, project(): pl.pallas_call(proj_kernel, grid=(toks // BLK,), in_specs=[pl.BlockSpec((...  57.5 us
    ppermute x59, starting transfers between devices, swap(): return lax.ppermute(x, SEQ_AXIS, [(d, d ^ dist) for d in range(n_dev)])  56.3 us
    dot_general x3, matrix products, back(): lax.dot_general(n_all[b], dlin, (((0,), (0,)), ((), ())), preferred_eleme...  47.1 us
    pallas_call x1, Pallas kernels, own_lin(): pl.pallas_call(lin_kernel, grid=(groups,), in_specs=[pl.BlockSpec((toks,...  32.5 us
  transfers between devices with their start and end apart: 66, of which 23 were waited for; matrix products, arithmetic and copies ran while one was open for 20% of the time, Pallas kernels for 44%

commit v1 on v0

--- a/solution.py
+++ b/solution.py
@@ -424,20 +424,21 @@
 
         o_cat = alloc((n_batch * seq_dev, n_dev * 2 * HD), BF16)
         o_cat = take_o(0, o_cat, saved[2][1])
-        drot0, dqg0, dkg0, dw0 = back(0, ())
-        o_cat = take_o(1, o_cat, drot0)
-        o_cat = take_o(2, o_cat, drot0)
+        o_cat = take_o(1, o_cat, saved[2][1])
+        o_cat = take_o(2, o_cat, ())
         part = lax.dot_general(o_cat, gy_cat, (((0,), (0,)), ((), ())), preferred_element_type=F32)
         grad_w_out = lax.psum_scatter(part, SEQ_AXIS, scatter_dimension=0, tiled=True)
-        drot1, dqg1, dkg1, dw1 = back(1, (part, dw0))
+        drot0, dqg0, dkg0, dw0 = back(0, part)
+        drot1, dqg1, dkg1, dw1 = back(1, dw0)
         dw01 = dw0 + dw1
         y_out = (x32.reshape(n_batch * seq_dev, dim) + dot_nn(after(o_cat, dw01), w_out)).astype(BF16).reshape(x_in.shape)
         grad_w_out = lax.all_gather(after(grad_w_out, (y_out, dw01)), SEQ_AXIS, axis=0, tiled=True)
         got0 = take_drot(drot0, drot1)
         drot2, dqg2, dkg2, dw2 = back(2, (dw01, y_out))
-        dw_sum = dw01 + dw2
+        dw_sum, grad_w_out = lax.optimization_barrier((dw01 + dw2, grad_w_out))
+        dw_q, dw_kv = dw_sum[:, :2 * HD], dw_sum[:, 2 * HD:]
         got1 = take_drot(drot1, drot2)
-        grad_x, dng0 = to_tokens(0, after(got0, dw_sum), None)
+        grad_x, dng0 = to_tokens(0, after(got0, (dw_q, dw_kv)), None)
         grad_x, dng1 = to_tokens(1, got1, grad_x)
         grad_x, dng2 = to_tokens(2, take_drot(drot2, grad_x), grad_x)
         dng_sum, dqg_sum, dkg_sum = dng0 + dng1 + dng2, dqg0 + dqg1 + dqg2, dkg0 + dkg1 + dkg2
@@ -445,9 +446,8 @@
         def gather_cols(own):
             return jnp.moveaxis(lax.all_gather(own, SEQ_AXIS, axis=0), 0, 1).reshape(dim, -1)
 
-        dw_sum, grad_w_out = lax.optimization_barrier((dw_sum, grad_w_out))
-        grad_w_query = gather_cols(dw_sum[:, :2 * HD])
-        dw_kv = lax.all_gather(after(dw_sum[:, 2 * HD:], dng0), SEQ_AXIS, axis=0)
+        grad_w_query = gather_cols(dw_q)
+        dw_kv = lax.all_gather(after(dw_kv, dng1), SEQ_AXIS, axis=0)
         grad_w_key = jnp.moveaxis(dw_kv[:, :, :HD], 0, 1).reshape(dim, -1)
         grad_w_value = jnp.moveaxis(dw_kv[:, :, HD:], 0, 1).reshape(dim, -1)
 

time: 1140 us -> 1360 us (1.19)
  waiting for transfers between devices: 271 us -> 482 us
  local copies, waits for them, and re-layouts: 143 us -> 162 us
    ppermute x59, waiting for transfers between devices: 206 us -> 301 us  [swap(): return lax.ppermute(x, SEQ_AXIS, [(d, d ^ dist) for d in range(n_dev)])]
    all_gather x3, waiting for transfers between devices: 32.2 us -> 107 us  [device_fn(): lax.all_gather(normed[b], SEQ_AXIS, axis=0, tiled=True)]
    all_gather x1, waiting for transfers between devices: 30.3 us -> 69.9 us  [gather_cols(): lax.all_gather(own, SEQ_AXIS, axis=0)]
  transfers between devices with their start and end apart: 66 -> 66, of which waited for: 23 -> 30; matrix products, arithmetic and copies ran while one was open for 20% -> 17% of each run, Pallas kernels for 44% -> 32%
where the time goes in v1:
time: 1360 us
  Pallas kernels  494 us (36%)
  waiting for transfers between devices  482 us (35%)
  local copies, waits for them, and re-layouts  162 us (12%)
  matrix products  103 us (8%)
  starting transfers between devices  51 us (4%)
  other arithmetic  48.4 us (4%)
  between operations  15.3 us (1%)
    ppermute x59, waiting for transfers between devices, swap(): return lax.ppermute(x, SEQ_AXIS, [(d, d ^ dist) for d in range(n_dev)])  301 us
    pallas_call x3, Pallas kernels, attend_back(): pl.pallas_call(bwd_kernel, grid=(toks // BLK,), in_specs=[whole(q), whole...  195 us
    pallas_call x3, Pallas kernels, attend(): pl.pallas_call(fwd_kernel, grid=(toks // BLK,), in_specs=[pl.BlockSpec((2...  118 us
    all_gather x3, waiting for transfers between devices, device_fn(): lax.all_gather(normed[b], SEQ_AXIS, axis=0, tiled=True)  107 us
    pallas_call x3, Pallas kernels, grad_tokens(): pl.pallas_call(gradx_kernel, grid=(groups,), in_specs=[pl.BlockSpec((1, t...  90.1 us
    all_gather x1, waiting for transfers between devices, gather_cols(): lax.all_gather(own, SEQ_AXIS, axis=0)  69.9 us
    pallas_call x3, Pallas kernels, project(): pl.pallas_call(proj_kernel, grid=(toks // BLK,), in_specs=[pl.BlockSpec((...  57.8 us
    ppermute x59, starting transfers between devices, swap(): return lax.ppermute(x, SEQ_AXIS, [(d, d ^ dist) for d in range(n_dev)])  50.3 us
  transfers between devices with their start and end apart: 66, of which 30 were waited for; matrix products, arithmetic and copies ran while one was open for 17% of the time, Pallas kernels for 32%

profile of v1, /device:TPU:0, one launch (start us, length us, event | category | flops | bytes accessed | tf_op | source)
XLA Modules:
  0.0 1355.4 jit_solution(13656925443388887021)
XLA Ops:
  13.1 4.1 multiply_reduce_fusion
  17.3 7.0 multiply_convert_fusion
  24.9 2.6 collective-permute-start.5
  31.5 5.8 fusion.17
  44.9 17.5 %convolution_convert_fusion = bf16[1536,2048]{1,0:T(8,128)(2,1)} fusion(bf16[1536,2048]{1,0:T(8,128)(2,1)S(1)} %bitcast.137, bf16[2048,2048]{1,0:T(8,128)(2,1)} %param.17), kind=kOutput, calls=%fused_computation.10 | convolution fusion | flops 12888047616 | bytes 20971520 | tf_op jit(solution)/shard_map/dot_general | solution.py:26
  62.4 22.3 %fusion.1 = (f32[3,4096,64]{2,1,0:T(8,128)S(1)}, f32[3,4096,64]{2,1,0:T(8,128)S(1)}, f32[3,4096,64]{2,1,0:T(8,128)S(1)}) fusion(f32[64]{0:T(128)S(1)} %multiply_power_fusion, f32[3,4096]{1,0:T(4,128)S(1)} %convert_element_type.26), kind=kLoop, calls=%fused_computation.22 | loop fusion | flops 1572864 | bytes 9486592 | tf_op jit(solution)/shard_map/neg | solution.py:338
  84.8 6.4 pad_maximum_fusion
  91.2 29.6 %all-gather.14.cloned.1.call-done = bf16[1,4096,2048]{2,1,0:T(8,128)(2,1)} async-done(((bf16[1,512,2048]{2,1,0:T(8,128)(2,1)}), bf16[1,4096,2048]{2,1,0:T(8,128)(2,1)}) %all-gather.14.cloned.1.call-update) | async-done | bytes 16777232 | tf_op jit(solution)/shard_map/all_gather | solution.py:367
  120.8 6.3 slice_bitcast_fusion.2
  127.0 3.2 slice_bitcast_fusion.3
  130.2 77.2 %all-gather.16.cloned.1.call-done = bf16[1,4096,2048]{2,1,0:T(8,128)(2,1)} async-done(((bf16[1,512,2048]{2,1,0:T(8,128)(2,1)}), bf16[1,4096,2048]{2,1,0:T(8,128)(2,1)}) %all-gather.16.cloned.1.call-update) | async-done | bytes 16777232 | tf_op jit(solution)/shard_map/all_gather | solution.py:367
  207.4 19.6 %proj.4 = (bf16[4096,256]{1,0:T(8,128)(2,1)}, bf16[256,4096]{1,0:T(8,128)(2,1)}, bf16[4096,128]{1,0:T(8,128)(2,1)}, bf16[128,4096]{1,0:T(8,128)(2,1)}, bf16[4096...) custom-call(bf16[4096,2048]{1,0:T(8,128)(2,1)} %bitcast.156, ...), custom_call_target="tpu_custom_call" | custom-call | flops 8589934592 | bytes 30000000 | tf_op jit(solution)/shard_map/proj/pallas_call | solution.py:69
  227.0 39.6 %attend.4 = (bf16[4096,256]{1,0:T(8,128)(2,1)}, f32[256,4096]{1,0:T(8,128)}, f32[2,4096]{1,0:T(2,128)}) custom-call(bf16[256,4096]{1,0:T(8,128)(2,1)} %get-tuple-element.153.qt_ref, bf16[4096,128]{1,0:T(8,128)(2,1)} %get-tuple-element.154.k_ref, bf16[128,4096]{1,0:T(8,128)(2,1)} %get-tuple-element.155.vt_ref), custom_call_target="tpu_custom_call" | custom-call | flops 17179869184 | bytes 10000000 | tf_op jit(solution)/shard_map/attend/pallas_call | solution.py:136
  266.6 19.1 %proj.3 = (bf16[4096,256]{1,0:T(8,128)(2,1)}, bf16[256,4096]{1,0:T(8,128)(2,1)}, bf16[4096,128]{1,0:T(8,128)(2,1)}, bf16[128,4096]{1,0:T(8,128)(2,1)}, bf16[4096...) custom-call(bf16[4096,2048]{1,0:T(8,128)(2,1)} %bitcast.157, ...), custom_call_target="tpu_custom_call" | custom-call | flops 8589934592 | bytes 30000000 | tf_op jit(solution)/shard_map/proj/pallas_call | solution.py:69
  285.7 39.2 %attend.3 = (bf16[4096,256]{1,0:T(8,128)(2,1)}, f32[256,4096]{1,0:T(8,128)}, f32[2,4096]{1,0:T(2,128)}) custom-call(bf16[256,4096]{1,0:T(8,128)(2,1)} %get-tuple-element.147.qt_ref, bf16[4096,128]{1,0:T(8,128)(2,1)} %get-tuple-element.148.k_ref, bf16[128,4096]{1,0:T(8,128)(2,1)} %get-tuple-element.149.vt_ref), custom_call_target="tpu_custom_call" | custom-call | flops 17179869184 | bytes 10000000 | tf_op jit(solution)/shard_map/attend/pallas_call | solution.py:136
  324.9 32.6 %own_lin.1.lin_ref = f32[8,1536,384]{2,1,0:T(8,128)} custom-call(bf16[1536,2048]{1,0:T(8,128)(2,1)} %bitcast.141, bf16[2048,2048]{1,0:T(8,128)(2,1)} %wq_ref.7, bf16[2048,1024]{1,0:T(8,128)(2,1)} %wk_ref.7), custom_call_target="tpu_custom_call" | custom-call | flops 19327352832 | bytes 60000000 | tf_op jit(solution)/shard_map/own_lin/pallas_call | solution.py:259
  362.3 19.0 %proj.5 = (bf16[4096,256]{1,0:T(8,128)(2,1)}, bf16[256,4096]{1,0:T(8,128)(2,1)}, bf16[4096,128]{1,0:T(8,128)(2,1)}, bf16[128,4096]{1,0:T(8,128)(2,1)}, bf16[4096...) custom-call(bf16[4096,2048]{1,0:T(8,128)(2,1)} %bitcast.158, ...), custom_call_target="tpu_custom_call" | custom-call | flops 8589934592 | bytes 30000000 | tf_op jit(solution)/shard_map/proj/pallas_call | solution.py:69
  382.9 39.4 %attend.5 = (bf16[4096,256]{1,0:T(8,128)(2,1)}, f32[256,4096]{1,0:T(8,128)}, f32[2,4096]{1,0:T(2,128)}) custom-call(bf16[256,4096]{1,0:T(8,128)(2,1)} %get-tuple-element.168.qt_ref, bf16[4096,128]{1,0:T(8,128)(2,1)} %get-tuple-element.169.k_ref, bf16[128,4096]{1,0:T(8,128)(2,1)} %get-tuple-element.170.vt_ref), custom_call_target="tpu_custom_call" | custom-call | flops 17179869184 | bytes 10000000 | tf_op jit(solution)/shard_map/attend/pallas_call | solution.py:136
  422.4 2.7 constant_dynamic-slice_fusion.40
  430.0 4.7 collective-permute-done.27
  436.7 3.8 collective-permute-done.15
  440.5 5.1 collective-permute-done.16
  448.4 3.3 collective-permute-done.19
  452.4 4.7 collective-permute-done.20
  457.2 16.8 %collective-permute-done.10 = bf16[512,256]{1,0:T(8,128)(2,1)S(1)} collective-permute-done((bf16[512,256]{1,0:T(8,128)(2,1)S(1)}, bf16[512,256]{1,0:T(8,128)(2,1)S(1)}, u32[]{:S(2)}, u32[]{:S(2)}) %collective-permute-start.10) | collective-permute-done | bytes 262176 | tf_op jit(solution)/shard_map/ppermute | solution.py:347
  474.7 4.8 collective-permute-done.11
  482.6 6.1 collective-permute-done.9
  522.3 18.8 %fusion.20 = f32[2048,2048]{1,0:T(8,128)} fusion(bf16[1536,2048]{1,0:T(8,128)(2,1)} %constant_dynamic-update-slice_fusion.24, bf16[1536,2048]{1,0:T(8,128)(2,1)S(1)} %bitcast.140), kind=kOutput, calls=%fused_computation.186 | convolution fusion | flops 12884901888 | bytes 29360128 | tf_op jit(solution)/shard_map/dot_general | solution.py:429
  541.3 4.9 constant_dynamic-slice_fusion.24
  550.9 15.9 %collective-permute-done.29 = bf16[1536,256]{1,0:T(8,128)(2,1)S(1)} collective-permute-done((bf16[1536,256]{1,0:T(8,128)(2,1)S(1)}, bf16[1536,256]{1,0:T(8,128)(2,1)S(1)}, u32[]{:S(2)}, u32[]{:S(2)}) %collective-permute-start.29) | collective-permute-done | bytes 786464 | tf_op jit(solution)/shard_map/ppermute | solution.py:347
  567.6 23.5 %collective-permute-done.30 = bf16[1536,256]{1,0:T(8,128)(2,1)} collective-permute-done((bf16[1536,256]{1,0:T(8,128)(2,1)}, bf16[1536,256]{1,0:T(8,128)(2,1)}, u32[]{:S(2)}, u32[]{:S(2)}) %collective-permute-start.30) | collective-permute-done | bytes 786464 | tf_op jit(solution)/shard_map/ppermute | solution.py:347
  591.2 8.0 collective-permute-done.32
  599.1 27.7 %collective-permute-done.33 = bf16[1536,256]{1,0:T(8,128)(2,1)} collective-permute-done((bf16[1536,256]{1,0:T(8,128)(2,1)S(1)}, bf16[1536,256]{1,0:T(8,128)(2,1)}, u32[]{:S(2)}, u32[]{:S(2)}) %collective-permute-start.33) | collective-permute-done | bytes 786464 | tf_op jit(solution)/shard_map/ppermute | solution.py:347
  626.8 30.9 %collective-permute-done.34 = bf16[1536,256]{1,0:T(8,128)(2,1)} collective-permute-done((bf16[1536,256]{1,0:T(8,128)(2,1)S(1)}, bf16[1536,256]{1,0:T(8,128)(2,1)}, u32[]{:S(2)}, u32[]{:S(2)}) %collective-permute-start.34) | collective-permute-done | bytes 786464 | tf_op jit(solution)/shard_map/ppermute | solution.py:347
  673.3 65.4 %attend_back.3 = (bf16[4096,512]{1,0:T(8,128)(2,1)}, bf16[4096,512]{1,0:T(8,128)(2,1)}, f32[1,128]{1,0:T(1,128)}, f32[1,128]{1,0:T(1,128)}) custom-call(bf16[4096,256]{1,0:T(8,128)(2,1)} %get-tuple-element.194.q_ref, bf16[256,4096]{1,0:T(8,128)(2,1)} %get-tuple-element.147.qt_ref, bf16[3,4096,256]{2,1,0:T(8,128)(2,1)} %constant_dynamic-update-slice_fusion.do_ref, ...), custom_call_target="tpu_custom_call" | custom-call | flops 42949672960 | bytes 20000000 | tf_op jit(solution)/shard_map/attend_back/pallas_call | solution.py:231
  738.7 15.0 %fusion.15 = f32[2048,512]{1,0:T(8,128)} fusion(bf16[4096,512]{1,0:T(8,128)(2,1)} %get-tuple-element.211, bf16[1,4096,2048]{2,1,0:T(8,128)(2,1)} %all-gather.14.cloned.1.call-done), kind=kOutput, calls=%fused_computation.181 | convolution fusion | flops 8589934592 | bytes 25165824 | tf_op jit(solution)/shard_map/dot_general | solution.py:418
  753.7 64.8 %attend_back.4 = (bf16[4096,512]{1,0:T(8,128)(2,1)}, bf16[4096,512]{1,0:T(8,128)(2,1)}, f32[1,128]{1,0:T(1,128)}, f32[1,128]{1,0:T(1,128)}) custom-call(bf16[4096,256]{1,0:T(8,128)(2,1)} %get-tuple-element.213.q_ref, bf16[256,4096]{1,0:T(8,128)(2,1)} %get-tuple-element.168.qt_ref, bf16[3,4096,256]{2,1,0:T(8,128)(2,1)} %constant_dynamic-update-slice_fusion.do_ref, ...), custom_call_target="tpu_custom_call" | custom-call | flops 42949672960 | bytes 20000000 | tf_op jit(solution)/shard_map/attend_back/pallas_call | solution.py:231
  818.4 16.0 %convolution_add_fusion.1 = f32[2048,512]{1,0:T(8,128)} fusion(f32[2048,512]{1,0:T(8,128)} %fusion.15, bf16[4096,512]{1,0:T(8,128)(2,1)} %get-tuple-element.218, bf16[1,4096,2048]{2,1,0:T(8,128)(2,1)} %all-gather.18.cloned.1.call-done), kind=kOutput, calls=%fused_computation.14 | convolution fusion | flops 8590983168 | bytes 29360128 | tf_op jit(solution)/shard_map/dot_general | solution.py:418
  834.4 20.1 %fusion = bf16[1536,2048]{1,0:T(8,128)(2,1)} fusion(bf16[1536,2048]{1,0:T(8,128)(2,1)} %constant_dynamic-update-slice_fusion.24, bf16[2048,2048]{1,0:T(8,128)(2,1)} %param.17, bf16[3,512,2048]{2,1,0:T(8,128)(2,1)} %x_ref.5), kind=kOutput, calls=%fused_computation.1 | convolution fusion | flops 12894339072 | bytes 27262976 | tf_op jit(solution)/shard_map/dot_general | solution.py:22
  854.9 4.0 constant_dynamic-slice_fusion
  863.9 2.8 multiply_sine_fusion.1
  868.9 4.0 constant_dynamic-slice_fusion.8
  874.3 12.3 collective-permute-done.50
  886.6 21.0 %collective-permute-done.51 = bf16[512,512]{1,0:T(8,128)(2,1)S(1)} collective-permute-done((bf16[512,512]{1,0:T(8,128)(2,1)}, bf16[512,512]{1,0:T(8,128)(2,1)S(1)}, u32[]{:S(2)}, u32[]{:S(2)}) %collective-permute-start.51) | collective-permute-done | bytes 524320 | tf_op jit(solution)/shard_map/ppermute | solution.py:347
  910.2 64.8 %attend_back.5 = (bf16[4096,512]{1,0:T(8,128)(2,1)}, bf16[4096,512]{1,0:T(8,128)(2,1)}, f32[1,128]{1,0:T(1,128)}, f32[1,128]{1,0:T(1,128)}) custom-call(bf16[4096,256]{1,0:T(8,128)(2,1)} %get-tuple-element.221.q_ref, bf16[256,4096]{1,0:T(8,128)(2,1)} %get-tuple-element.153.qt_ref, bf16[3,4096,256]{2,1,0:T(8,128)(2,1)} %constant_dynamic-update-slice_fusion.do_ref, ...), custom_call_target="tpu_custom_call" | custom-call | flops 42949672960 | bytes 20000000 | tf_op jit(solution)/shard_map/attend_back/pallas_call | solution.py:231
  979.9 15.6 %convolution_add_fusion = f32[2048,512]{1,0:T(8,128)} fusion(f32[2048,512]{1,0:T(8,128)} %convolution_add_fusion.1, bf16[4096,512]{1,0:T(8,128)(2,1)} %get-tuple-element.251, bf16[1,4096,2048]{2,1,0:T(8,128)(2,1)} %all-gather.16.cloned.1.call-done), kind=kOutput, calls=%fused_computation.13 | convolution fusion | flops 8590983168 | bytes 29360128 | tf_op jit(solution)/shard_map/dot_general | solution.py:418
  995.4 3.2 collective-permute-done.44
  998.6 29.3 %collective-permute-done.46 = bf16[512,512]{1,0:T(8,128)(2,1)S(1)} collective-permute-done((bf16[512,512]{1,0:T(8,128)(2,1)}, bf16[512,512]{1,0:T(8,128)(2,1)S(1)}, u32[]{:S(2)}, u32[]{:S(2)}) %collective-permute-start.46) | collective-permute-done | bytes 524320 | tf_op jit(solution)/shard_map/ppermute | solution.py:347
  1045.3 4.5 fusion.18
  1049.8 30.2 %grad_tokens.3 = (bf16[3,512,2048]{2,1,0:T(8,128)(2,1)}, f32[1,2048]{1,0:T(1,128)}) custom-call(bf16[8,512,512]{2,1,0:T(8,128)(2,1)} %bitcast_dynamic-update-slice_fusion.8.drot_ref, f32[8,1536,384]{2,1,0:T(8,128)} %own_lin.1.lin_ref, bf16[2048,2048]{1,0:T(8,128)(2,1)} %wq_ref.7, bf16[2048,1024]{1,0:T(8,128)(2,1)} %wk_ref.7, bf16[2048,1024]{1,0:T(8,128)(2,1)} %wv_ref.5, ...), custom_call_target="tpu_custom_call" | custom-call | flops 8589934592 | bytes 40000000 | tf_op jit(solution)/shard_map/grad_tokens/pallas_call | solution.py:310
  1080.0 29.9 %grad_tokens.4 = (bf16[3,512,2048]{2,1,0:T(8,128)(2,1)}, f32[1,2048]{1,0:T(1,128)}) custom-call(bf16[8,512,512]{2,1,0:T(8,128)(2,1)} %bitcast_dynamic-update-slice_fusion.16.drot_ref, f32[8,1536,384]{2,1,0:T(8,128)} %own_lin.1.lin_ref, bf16[2048,2048]{1,0:T(8,128)(2,1)} %wq_ref.7, bf16[2048,1024]{1,0:T(8,128)(2,1)} %wk_ref.7, ...), custom_call_target="tpu_custom_call", output_to_operand_aliasing={{0}: (12, {})} | custom-call | flops 8589934592 | bytes 40000000 | tf_op jit(solution)/shard_map/grad_tokens/pallas_call | solution.py:310
  1110.8 3.8 constant_dynamic-slice_fusion.16
  1119.4 20.5 %collective-permute-done.36 = bf16[512,512]{1,0:T(8,128)(2,1)S(1)} collective-permute-done((bf16[512,512]{1,0:T(8,128)(2,1)S(1)}, bf16[512,512]{1,0:T(8,128)(2,1)S(1)}, u32[]{:S(2)}, u32[]{:S(2)}) %collective-permute-start.36) | collective-permute-done | bytes 524320 | tf_op jit(solution)/shard_map/ppermute | solution.py:347
  1140.0 21.9 %collective-permute-done.37 = bf16[512,512]{1,0:T(8,128)(2,1)S(1)} collective-permute-done((bf16[512,512]{1,0:T(8,128)(2,1)}, bf16[512,512]{1,0:T(8,128)(2,1)S(1)}, u32[]{:S(2)}, u32[]{:S(2)}) %collective-permute-start.37) | collective-permute-done | bytes 524320 | tf_op jit(solution)/shard_map/ppermute | solution.py:347
  1161.9 24.7 %collective-permute-done.39 = bf16[512,512]{1,0:T(8,128)(2,1)S(1)} collective-permute-done((bf16[512,512]{1,0:T(8,128)(2,1)}, bf16[512,512]{1,0:T(8,128)(2,1)S(1)}, u32[]{:S(2)}, u32[]{:S(2)}) %collective-permute-start.39) | collective-permute-done | bytes 524320 | tf_op jit(solution)/shard_map/ppermute | solution.py:347
  1195.5 30.0 %grad_tokens.5 = (bf16[3,512,2048]{2,1,0:T(8,128)(2,1)}, f32[1,2048]{1,0:T(1,128)}) custom-call(bf16[8,512,512]{2,1,0:T(8,128)(2,1)} %bitcast_dynamic-update-slice_fusion.drot_ref, f32[8,1536,384]{2,1,0:T(8,128)} %own_lin.1.lin_ref, bf16[2048,2048]{1,0:T(8,128)(2,1)} %wq_ref.7, bf16[2048,1024]{1,0:T(8,128)(2,1)} %wk_ref.7, ...), custom_call_target="tpu_custom_call", output_to_operand_aliasing={{0}: (12, {})} | custom-call | flops 8589934592 | bytes 40000000 | tf_op jit(solution)/shard_map/grad_tokens/pallas_call | solution.py:310
  1232.0 3.6 collective-permute-done.58
  1236.8 2.6 all-gather.22.cloned.1.call-done
  1239.4 6.7 slice_bitcast_fusion
  1246.1 4.8 copy.29
  1250.9 4.6 copy.30
  1255.5 69.9 %all-gather.20.cloned.1.call-done = f32[16384,256]{1,0:T(8,128)} async-done(((f32[2048,256]{1,0:T(8,128)}), f32[16384,256]{1,0:T(8,128)}) %all-gather.20.cloned.1.call-update) | async-done | bytes 16777232 | tf_op jit(solution)/shard_map/all_gather | solution.py:447
  1325.4 13.8 %copy.24 = f32[8,256,8,256]{3,2,0,1:T(8,128)} copy(f32[8,256,8,256]{3,2,1,0:T(8,128)} %bitcast.144) | data formatting | bytes 33554432 | tf_op jit(solution)/shard_map/reshape | solution.py:447
  1341.9 6.2 copy.98
  (284 shorter events, 152.0 us)
Async XLA Ops:
  7.2 113.6 %all-gather.14.cloned.1.call-start = ((), (), s32[]{:S(2)}) async-start(), calls=%async_computation.3 | async-start | bytes 18874368 | tf_op jit(solution)/shard_map/all_gather | solution.py:367
  7.2 17.7 %collective-permute-start = (s32[3,512]{1,0:T(4,128)}, s32[3,512]{1,0:T(4,128)S(1)}, u32[]{:S(2)}, u32[]{:S(2)}) collective-permute-start(s32[3,512]{1,0:T(4,128)} %param.12), channel_id=1, source_target_pairs={{0,1},{1,0},{2,3},{3,2},{4,5},{5,4},{6,7},{7,6}} | collective-permute-start | bytes 18440 | tf_op jit(solution)/shard_map/ppermute | solution.py:347
  8.1 19.4 %collective-permute-start.1 = (s32[3,512]{1,0:T(4,128)}, s32[3,512]{1,0:T(4,128)S(1)}, u32[]{:S(2)}, u32[]{:S(2)}) collective-permute-start(s32[3,512]{1,0:T(4,128)} %param.12), channel_id=1, source_target_pairs={{0,2},{1,3},{2,0},{3,1},{4,6},{5,7},{6,4},{7,5}} | collective-permute-start | bytes 18440 | tf_op jit(solution)/shard_map/ppermute | solution.py:347
  10.6 17.0 %collective-permute-start.2 = (s32[3,512]{1,0:T(4,128)}, s32[3,512]{1,0:T(4,128)S(1)}, u32[]{:S(2)}, u32[]{:S(2)}) collective-permute-start(s32[3,512]{1,0:T(4,128)} %param.12), channel_id=1, source_target_pairs={{0,3},{1,2},{2,1},{3,0},{4,7},{5,6},{6,5},{7,4}} | collective-permute-start | bytes 18440 | tf_op jit(solution)/shard_map/ppermute | solution.py:347
  10.7 17.0 %collective-permute-start.3 = (s32[3,512]{1,0:T(4,128)}, s32[3,512]{1,0:T(4,128)S(1)}, u32[]{:S(2)}, u32[]{:S(2)}) collective-permute-start(s32[3,512]{1,0:T(4,128)} %param.12), channel_id=1, source_target_pairs={{0,4},{1,5},{2,6},{3,7},{4,0},{5,1},{6,2},{7,3}} | collective-permute-start | bytes 18440 | tf_op jit(solution)/shard_map/ppermute | solution.py:347
  12.4 15.2 %collective-permute-start.4 = (s32[3,512]{1,0:T(4,128)}, s32[3,512]{1,0:T(4,128)S(1)}, u32[]{:S(2)}, u32[]{:S(2)}) collective-permute-start(s32[3,512]{1,0:T(4,128)} %param.12), channel_id=1, source_target_pairs={{0,5},{1,4},{2,7},{3,6},{4,1},{5,0},{6,3},{7,2}} | collective-permute-start | bytes 18440 | tf_op jit(solution)/shard_map/ppermute | solution.py:347
  24.9 4.6 collective-permute-start.5
  27.5 4.0 collective-permute-start.6
  37.3 170.0 %all-gather.16.cloned.1.call-start = ((), (), s32[]{:S(2)}) async-start(), calls=%async_computation.4 | async-start | bytes 18874368 | tf_op jit(solution)/shard_map/all_gather | solution.py:367
  38.1 319.5 %all-gather.18.cloned.1.call-start = ((), (), s32[]{:S(2)}) async-start(), calls=%async_computation.5 | async-start | bytes 18874368 | tf_op jit(solution)/shard_map/all_gather | solution.py:367
  38.8 815.7 %reduce-scatter.2.cloned.1.call-start = ((), (), s32[]{:S(2)}) async-start(), calls=%async_computation.1 | async-start | bytes 18874368 | tf_op jit(solution)/shard_map/reduce_scatter | solution.py:430
  358.6 22.7 %collective-permute-start.21 = (bf16[512,256]{1,0:T(8,128)(2,1)S(1)}, bf16[512,256]{1,0:T(8,128)(2,1)S(1)}, u32[]{:S(2)}, u32[]{:S(2)}) collective-permute-start(bf16[512,256]{1,0:T(8,128)(2,1)S(1)} %get-tuple-element.328), channel_id=1, source_target_pairs={{0,1},{1,0},{2,3},{3,2},{4,5},{5,4},{6,7},{7,6}} | collective-permute-start | bytes 786440 | tf_op jit(solution)/shard_map/ppermute | solution.py:347
  358.8 66.3 %collective-permute-start.22 = (bf16[512,256]{1,0:T(8,128)(2,1)}, bf16[512,256]{1,0:T(8,128)(2,1)}, u32[]{:S(2)}, u32[]{:S(2)}) collective-permute-start(bf16[512,256]{1,0:T(8,128)(2,1)} %get-tuple-element.327), channel_id=1, source_target_pairs={{0,2},{1,3},{2,0},{3,1},{4,6},{5,7},{6,4},{7,5}} | collective-permute-start | bytes 786440 | tf_op jit(solution)/shard_map/ppermute | solution.py:347
  360.2 65.9 %collective-permute-start.23 = (bf16[512,256]{1,0:T(8,128)(2,1)}, bf16[512,256]{1,0:T(8,128)(2,1)}, u32[]{:S(2)}, u32[]{:S(2)}) collective-permute-start(bf16[512,256]{1,0:T(8,128)(2,1)} %get-tuple-element.326), channel_id=1, source_target_pairs={{0,3},{1,2},{2,1},{3,0},{4,7},{5,6},{6,5},{7,4}} | collective-permute-start | bytes 786440 | tf_op jit(solution)/shard_map/ppermute | solution.py:347
  360.4 66.1 %collective-permute-start.24 = (bf16[512,256]{1,0:T(8,128)(2,1)}, bf16[512,256]{1,0:T(8,128)(2,1)}, u32[]{:S(2)}, u32[]{:S(2)}) collective-permute-start(bf16[512,256]{1,0:T(8,128)(2,1)} %get-tuple-element.325), channel_id=1, source_target_pairs={{0,4},{1,5},{2,6},{3,7},{4,0},{5,1},{6,2},{7,3}} | collective-permute-start | bytes 786440 | tf_op jit(solution)/shard_map/ppermute | solution.py:347
  361.4 66.6 %collective-permute-start.25 = (bf16[512,256]{1,0:T(8,128)(2,1)}, bf16[512,256]{1,0:T(8,128)(2,1)}, u32[]{:S(2)}, u32[]{:S(2)}) collective-permute-start(bf16[512,256]{1,0:T(8,128)(2,1)} %get-tuple-element.324), channel_id=1, source_target_pairs={{0,5},{1,4},{2,7},{3,6},{4,1},{5,0},{6,3},{7,2}} | collective-permute-start | bytes 786440 | tf_op jit(solution)/shard_map/ppermute | solution.py:347
  381.3 46.7 %collective-permute-start.26 = (bf16[512,256]{1,0:T(8,128)(2,1)S(1)}, bf16[512,256]{1,0:T(8,128)(2,1)}, u32[]{:S(2)}, u32[]{:S(2)}) collective-permute-start(bf16[512,256]{1,0:T(8,128)(2,1)S(1)} %get-tuple-element.323), channel_id=1, source_target_pairs={{0,6},{1,7},{2,4},{3,5},{4,2},{5,3},{6,0},{7,1}} | collective-permute-start | bytes 786440 | tf_op jit(solution)/shard_map/ppermute | solution.py:347
  425.1 9.6 collective-permute-start.27
  426.1 9.7 collective-permute-start.14
  426.6 13.9 %collective-permute-start.15 = (bf16[512,256]{1,0:T(8,128)(2,1)}, bf16[512,256]{1,0:T(8,128)(2,1)}, u32[]{:S(2)}, u32[]{:S(2)}) collective-permute-start(bf16[512,256]{1,0:T(8,128)(2,1)} %get-tuple-element.335), channel_id=1, source_target_pairs={{0,2},{1,3},{2,0},{3,1},{4,6},{5,7},{6,4},{7,5}} | collective-permute-start | bytes 786440 | tf_op jit(solution)/shard_map/ppermute | solution.py:347
  428.0 17.6 %collective-permute-start.16 = (bf16[512,256]{1,0:T(8,128)(2,1)}, bf16[512,256]{1,0:T(8,128)(2,1)}, u32[]{:S(2)}, u32[]{:S(2)}) collective-permute-start(bf16[512,256]{1,0:T(8,128)(2,1)} %get-tuple-element.334), channel_id=1, source_target_pairs={{0,3},{1,2},{2,1},{3,0},{4,7},{5,6},{6,5},{7,4}} | collective-permute-start | bytes 786440 | tf_op jit(solution)/shard_map/ppermute | solution.py:347
  428.0 18.4 %collective-permute-start.17 = (bf16[512,256]{1,0:T(8,128)(2,1)}, bf16[512,256]{1,0:T(8,128)(2,1)}, u32[]{:S(2)}, u32[]{:S(2)}) collective-permute-start(bf16[512,256]{1,0:T(8,128)(2,1)} %get-tuple-element.333), channel_id=1, source_target_pairs={{0,4},{1,5},{2,6},{3,7},{4,0},{5,1},{6,2},{7,3}} | collective-permute-start | bytes 786440 | tf_op jit(solution)/shard_map/ppermute | solution.py:347
  434.7 12.7 collective-permute-start.18
  435.8 16.0 %collective-permute-start.19 = (bf16[512,256]{1,0:T(8,128)(2,1)}, bf16[512,256]{1,0:T(8,128)(2,1)S(1)}, u32[]{:S(2)}, u32[]{:S(2)}) collective-permute-start(bf16[512,256]{1,0:T(8,128)(2,1)} %get-tuple-element.331), channel_id=1, source_target_pairs={{0,6},{1,7},{2,4},{3,5},{4,2},{5,3},{6,0},{7,1}} | collective-permute-start | bytes 786440 | tf_op jit(solution)/shard_map/ppermute | solution.py:347
  440.5 16.6 %collective-permute-start.20 = (bf16[512,256]{1,0:T(8,128)(2,1)S(1)}, bf16[512,256]{1,0:T(8,128)(2,1)S(1)}, u32[]{:S(2)}, u32[]{:S(2)}) collective-permute-start(bf16[512,256]{1,0:T(8,128)(2,1)S(1)} %get-tuple-element.330), channel_id=1, source_target_pairs={{0,7},{1,6},{2,5},{3,4},{4,3},{5,2},{6,1},{7,0}} | collective-permute-start | bytes 786440 | tf_op jit(solution)/shard_map/ppermute | solution.py:347
  445.6 28.4 %collective-permute-start.10 = (bf16[512,256]{1,0:T(8,128)(2,1)S(1)}, bf16[512,256]{1,0:T(8,128)(2,1)S(1)}, u32[]{:S(2)}, u32[]{:S(2)}) collective-permute-start(bf16[512,256]{1,0:T(8,128)(2,1)S(1)} %get-tuple-element.341), channel_id=1, source_target_pairs={{0,4},{1,5},{2,6},{3,7},{4,0},{5,1},{6,2},{7,3}} | collective-permute-start | bytes 786440 | tf_op jit(solution)/shard_map/ppermute | solution.py:347
  446.4 33.1 %collective-permute-start.11 = (bf16[512,256]{1,0:T(8,128)(2,1)S(1)}, bf16[512,256]{1,0:T(8,128)(2,1)S(1)}, u32[]{:S(2)}, u32[]{:S(2)}) collective-permute-start(bf16[512,256]{1,0:T(8,128)(2,1)S(1)} %get-tuple-element.340), channel_id=1, source_target_pairs={{0,5},{1,4},{2,7},{3,6},{4,1},{5,0},{6,3},{7,2}} | collective-permute-start | bytes 786440 | tf_op jit(solution)/shard_map/ppermute | solution.py:347
  447.4 33.5 %collective-permute-start.12 = (bf16[512,256]{1,0:T(8,128)(2,1)}, bf16[512,256]{1,0:T(8,128)(2,1)}, u32[]{:S(2)}, u32[]{:S(2)}) collective-permute-start(bf16[512,256]{1,0:T(8,128)(2,1)} %get-tuple-element.339), channel_id=1, source_target_pairs={{0,6},{1,7},{2,4},{3,5},{4,2},{5,3},{6,0},{7,1}} | collective-permute-start | bytes 786440 | tf_op jit(solution)/shard_map/ppermute | solution.py:347
  451.8 29.1 %collective-permute-start.13 = (bf16[512,256]{1,0:T(8,128)(2,1)}, bf16[512,256]{1,0:T(8,128)(2,1)}, u32[]{:S(2)}, u32[]{:S(2)}) collective-permute-start(bf16[512,256]{1,0:T(8,128)(2,1)} %get-tuple-element.338), channel_id=1, source_target_pairs={{0,7},{1,6},{2,5},{3,4},{4,3},{5,2},{6,1},{7,0}} | collective-permute-start | bytes 786440 | tf_op jit(solution)/shard_map/ppermute | solution.py:347
  457.1 23.8 %collective-permute-start.7 = (bf16[512,256]{1,0:T(8,128)(2,1)}, bf16[512,256]{1,0:T(8,128)(2,1)}, u32[]{:S(2)}, u32[]{:S(2)}) collective-permute-start(bf16[512,256]{1,0:T(8,128)(2,1)} %get-tuple-element.344), channel_id=1, source_target_pairs={{0,1},{1,0},{2,3},{3,2},{4,5},{5,4},{6,7},{7,6}} | collective-permute-start | bytes 786440 | tf_op jit(solution)/shard_map/ppermute | solution.py:347
  474.0 8.5 collective-permute-start.8
  480.3 8.5 collective-permute-start.9
  541.2 504.2 %all-gather.12.cloned.1.call-start = ((), (), s32[]{:S(2)}) async-start(), calls=%async_computation.2 | async-start | bytes 18874368 | tf_op jit(solution)/shard_map/all_gather | solution.py:435
  546.3 20.4 %collective-permute-start.29 = (bf16[1536,256]{1,0:T(8,128)(2,1)S(1)}, bf16[1536,256]{1,0:T(8,128)(2,1)S(1)}, u32[]{:S(2)}, u32[]{:S(2)}) collective-permute-start(bf16[1536,256]{1,0:T(8,128)(2,1)S(1)} %get-tuple-element.284), channel_id=1, source_target_pairs={{0,2},{1,3},{2,0},{3,1},{4,6},{5,7},{6,4},{7,5}} | collective-permute-start | bytes 2359304 | tf_op jit(solution)/shard_map/ppermute | solution.py:347
  546.7 44.4 %collective-permute-start.30 = (bf16[1536,256]{1,0:T(8,128)(2,1)}, bf16[1536,256]{1,0:T(8,128)(2,1)}, u32[]{:S(2)}, u32[]{:S(2)}) collective-permute-start(bf16[1536,256]{1,0:T(8,128)(2,1)} %get-tuple-element.283), channel_id=1, source_target_pairs={{0,3},{1,2},{2,1},{3,0},{4,7},{5,6},{6,5},{7,4}} | collective-permute-start | bytes 2359304 | tf_op jit(solution)/shard_map/ppermute | solution.py:347
  548.0 43.1 %collective-permute-start.31 = (bf16[1536,256]{1,0:T(8,128)(2,1)}, bf16[1536,256]{1,0:T(8,128)(2,1)}, u32[]{:S(2)}, u32[]{:S(2)}) collective-permute-start(bf16[1536,256]{1,0:T(8,128)(2,1)} %get-tuple-element.282), channel_id=1, source_target_pairs={{0,4},{1,5},{2,6},{3,7},{4,0},{5,1},{6,2},{7,3}} | collective-permute-start | bytes 2359304 | tf_op jit(solution)/shard_map/ppermute | solution.py:347
  548.9 50.3 %collective-permute-start.32 = (bf16[1536,256]{1,0:T(8,128)(2,1)S(1)}, bf16[1536,256]{1,0:T(8,128)(2,1)}, u32[]{:S(2)}, u32[]{:S(2)}) collective-permute-start(bf16[1536,256]{1,0:T(8,128)(2,1)S(1)} %get-tuple-element.281), channel_id=1, source_target_pairs={{0,5},{1,4},{2,7},{3,6},{4,1},{5,0},{6,3},{7,2}} | collective-permute-start | bytes 2359304 | tf_op jit(solution)/shard_map/ppermute | solution.py:347
  549.8 77.0 %collective-permute-start.33 = (bf16[1536,256]{1,0:T(8,128)(2,1)S(1)}, bf16[1536,256]{1,0:T(8,128)(2,1)}, u32[]{:S(2)}, u32[]{:S(2)}) collective-permute-start(bf16[1536,256]{1,0:T(8,128)(2,1)S(1)} %get-tuple-element.280), channel_id=1, source_target_pairs={{0,6},{1,7},{2,4},{3,5},{4,2},{5,3},{6,0},{7,1}} | collective-permute-start | bytes 2359304 | tf_op jit(solution)/shard_map/ppermute | solution.py:347
  567.6 90.1 %collective-permute-start.34 = (bf16[1536,256]{1,0:T(8,128)(2,1)S(1)}, bf16[1536,256]{1,0:T(8,128)(2,1)}, u32[]{:S(2)}, u32[]{:S(2)}) collective-permute-start(bf16[1536,256]{1,0:T(8,128)(2,1)S(1)} %get-tuple-element.279), channel_id=1, source_target_pairs={{0,7},{1,6},{2,5},{3,4},{4,3},{5,2},{6,1},{7,0}} | collective-permute-start | bytes 2359304 | tf_op jit(solution)/shard_map/ppermute | solution.py:347
  854.5 384.8 %all-gather.22.cloned.1.call-start = ((), (), s32[]{:S(2)}) async-start(), calls=%async_computation.7 | async-start | bytes 18874368 | tf_op jit(solution)/shard_map/all_gather | solution.py:450
  859.0 14.0 %collective-permute-start.49 = (bf16[512,512]{1,0:T(8,128)(2,1)}, bf16[512,512]{1,0:T(8,128)(2,1)S(1)}, u32[]{:S(2)}, u32[]{:S(2)}) collective-permute-start(bf16[512,512]{1,0:T(8,128)(2,1)} %get-tuple-element.304), channel_id=1, source_target_pairs={{0,1},{1,0},{2,3},{3,2},{4,5},{5,4},{6,7},{7,6}} | collective-permute-start | bytes 1572872 | tf_op jit(solution)/shard_map/ppermute | solution.py:347
  861.0 25.6 %collective-permute-start.50 = (bf16[512,512]{1,0:T(8,128)(2,1)}, bf16[512,512]{1,0:T(8,128)(2,1)S(1)}, u32[]{:S(2)}, u32[]{:S(2)}) collective-permute-start(bf16[512,512]{1,0:T(8,128)(2,1)} %get-tuple-element.303), channel_id=1, source_target_pairs={{0,2},{1,3},{2,0},{3,1},{4,6},{5,7},{6,4},{7,5}} | collective-permute-start | bytes 1572872 | tf_op jit(solution)/shard_map/ppermute | solution.py:347
  861.6 46.0 %collective-permute-start.51 = (bf16[512,512]{1,0:T(8,128)(2,1)}, bf16[512,512]{1,0:T(8,128)(2,1)S(1)}, u32[]{:S(2)}, u32[]{:S(2)}) collective-permute-start(bf16[512,512]{1,0:T(8,128)(2,1)} %get-tuple-element.302), channel_id=1, source_target_pairs={{0,3},{1,2},{2,1},{3,0},{4,7},{5,6},{6,5},{7,4}} | collective-permute-start | bytes 1572872 | tf_op jit(solution)/shard_map/ppermute | solution.py:347
  862.3 46.9 %collective-permute-start.52 = (bf16[512,512]{1,0:T(8,128)(2,1)}, bf16[512,512]{1,0:T(8,128)(2,1)S(1)}, u32[]{:S(2)}, u32[]{:S(2)}) collective-permute-start(bf16[512,512]{1,0:T(8,128)(2,1)} %get-tuple-element.301), channel_id=1, source_target_pairs={{0,4},{1,5},{2,6},{3,7},{4,0},{5,1},{6,2},{7,3}} | collective-permute-start | bytes 1572872 | tf_op jit(solution)/shard_map/ppermute | solution.py:347
  868.3 106.6 %collective-permute-start.53 = (bf16[512,512]{1,0:T(8,128)(2,1)}, bf16[512,512]{1,0:T(8,128)(2,1)S(1)}, u32[]{:S(2)}, u32[]{:S(2)}) collective-permute-start(bf16[512,512]{1,0:T(8,128)(2,1)} %get-tuple-element.300), channel_id=1, source_target_pairs={{0,5},{1,4},{2,7},{3,6},{4,1},{5,0},{6,3},{7,2}} | collective-permute-start | bytes 1572872 | tf_op jit(solution)/shard_map/ppermute | solution.py:347
  873.0 102.5 %collective-permute-start.54 = (bf16[512,512]{1,0:T(8,128)(2,1)}, bf16[512,512]{1,0:T(8,128)(2,1)}, u32[]{:S(2)}, u32[]{:S(2)}) collective-permute-start(bf16[512,512]{1,0:T(8,128)(2,1)} %get-tuple-element.299), channel_id=1, source_target_pairs={{0,6},{1,7},{2,4},{3,5},{4,2},{5,3},{6,0},{7,1}} | collective-permute-start | bytes 1572872 | tf_op jit(solution)/shard_map/ppermute | solution.py:347
  886.6 90.5 %collective-permute-start.55 = (bf16[512,512]{1,0:T(8,128)(2,1)}, bf16[512,512]{1,0:T(8,128)(2,1)}, u32[]{:S(2)}, u32[]{:S(2)}) collective-permute-start(bf16[512,512]{1,0:T(8,128)(2,1)} %get-tuple-element.298), channel_id=1, source_target_pairs={{0,7},{1,6},{2,5},{3,4},{4,3},{5,2},{6,1},{7,0}} | collective-permute-start | bytes 1572872 | tf_op jit(solution)/shard_map/ppermute | solution.py:347
  907.6 70.0 %collective-permute-start.42 = (bf16[512,512]{1,0:T(8,128)(2,1)}, bf16[512,512]{1,0:T(8,128)(2,1)}, u32[]{:S(2)}, u32[]{:S(2)}) collective-permute-start(bf16[512,512]{1,0:T(8,128)(2,1)} %get-tuple-element.312), channel_id=1, source_target_pairs={{0,1},{1,0},{2,3},{3,2},{4,5},{5,4},{6,7},{7,6}} | collective-permute-start | bytes 1572872 | tf_op jit(solution)/shard_map/ppermute | solution.py:347
  909.3 69.5 %collective-permute-start.43 = (bf16[512,512]{1,0:T(8,128)(2,1)}, bf16[512,512]{1,0:T(8,128)(2,1)}, u32[]{:S(2)}, u32[]{:S(2)}) collective-permute-start(bf16[512,512]{1,0:T(8,128)(2,1)} %get-tuple-element.311), channel_id=1, source_target_pairs={{0,2},{1,3},{2,0},{3,1},{4,6},{5,7},{6,4},{7,5}} | collective-permute-start | bytes 1572872 | tf_op jit(solution)/shard_map/ppermute | solution.py:347
  975.0 23.7 %collective-permute-start.44 = (bf16[512,512]{1,0:T(8,128)(2,1)}, bf16[512,512]{1,0:T(8,128)(2,1)S(1)}, u32[]{:S(2)}, u32[]{:S(2)}) collective-permute-start(bf16[512,512]{1,0:T(8,128)(2,1)} %get-tuple-element.310), channel_id=1, source_target_pairs={{0,3},{1,2},{2,1},{3,0},{4,7},{5,6},{6,5},{7,4}} | collective-permute-start | bytes 1572872 | tf_op jit(solution)/shard_map/ppermute | solution.py:347
  975.4 23.2 %collective-permute-start.45 = (bf16[512,512]{1,0:T(8,128)(2,1)}, bf16[512,512]{1,0:T(8,128)(2,1)S(1)}, u32[]{:S(2)}, u32[]{:S(2)}) collective-permute-start(bf16[512,512]{1,0:T(8,128)(2,1)} %get-tuple-element.309), channel_id=1, source_target_pairs={{0,4},{1,5},{2,6},{3,7},{4,0},{5,1},{6,2},{7,3}} | collective-permute-start | bytes 1572872 | tf_op jit(solution)/shard_map/ppermute | solution.py:347
  977.1 50.8 %collective-permute-start.46 = (bf16[512,512]{1,0:T(8,128)(2,1)}, bf16[512,512]{1,0:T(8,128)(2,1)S(1)}, u32[]{:S(2)}, u32[]{:S(2)}) collective-permute-start(bf16[512,512]{1,0:T(8,128)(2,1)} %get-tuple-element.308), channel_id=1, source_target_pairs={{0,5},{1,4},{2,7},{3,6},{4,1},{5,0},{6,3},{7,2}} | collective-permute-start | bytes 1572872 | tf_op jit(solution)/shard_map/ppermute | solution.py:347
  977.6 50.3 %collective-permute-start.47 = (bf16[512,512]{1,0:T(8,128)(2,1)}, bf16[512,512]{1,0:T(8,128)(2,1)S(1)}, u32[]{:S(2)}, u32[]{:S(2)}) collective-permute-start(bf16[512,512]{1,0:T(8,128)(2,1)} %get-tuple-element.307), channel_id=1, source_target_pairs={{0,6},{1,7},{2,4},{3,5},{4,2},{5,3},{6,0},{7,1}} | collective-permute-start | bytes 1572872 | tf_op jit(solution)/shard_map/ppermute | solution.py:347
  978.8 49.1 %collective-permute-start.48 = (bf16[512,512]{1,0:T(8,128)(2,1)}, bf16[512,512]{1,0:T(8,128)(2,1)S(1)}, u32[]{:S(2)}, u32[]{:S(2)}) collective-permute-start(bf16[512,512]{1,0:T(8,128)(2,1)} %get-tuple-element.306), channel_id=1, source_target_pairs={{0,7},{1,6},{2,5},{3,4},{4,3},{5,2},{6,1},{7,0}} | collective-permute-start | bytes 1572872 | tf_op jit(solution)/shard_map/ppermute | solution.py:347
  1109.9 215.4 %all-gather.20.cloned.1.call-start = ((), (), s32[]{:S(2)}) async-start(), calls=%async_computation.6 | async-start | bytes 18874368 | tf_op jit(solution)/shard_map/all_gather | solution.py:447
  1114.6 3.6 collective-permute-start.35
  1114.7 25.2 %collective-permute-start.36 = (bf16[512,512]{1,0:T(8,128)(2,1)S(1)}, bf16[512,512]{1,0:T(8,128)(2,1)S(1)}, u32[]{:S(2)}, u32[]{:S(2)}) collective-permute-start(bf16[512,512]{1,0:T(8,128)(2,1)S(1)} %get-tuple-element.319), channel_id=1, source_target_pairs={{0,2},{1,3},{2,0},{3,1},{4,6},{5,7},{6,4},{7,5}} | collective-permute-start | bytes 1572872 | tf_op jit(solution)/shard_map/ppermute | solution.py:347
  1116.1 45.8 %collective-permute-start.37 = (bf16[512,512]{1,0:T(8,128)(2,1)}, bf16[512,512]{1,0:T(8,128)(2,1)S(1)}, u32[]{:S(2)}, u32[]{:S(2)}) collective-permute-start(bf16[512,512]{1,0:T(8,128)(2,1)} %get-tuple-element.318), channel_id=1, source_target_pairs={{0,3},{1,2},{2,1},{3,0},{4,7},{5,6},{6,5},{7,4}} | collective-permute-start | bytes 1572872 | tf_op jit(solution)/shard_map/ppermute | solution.py:347
  1116.4 45.5 %collective-permute-start.38 = (bf16[512,512]{1,0:T(8,128)(2,1)}, bf16[512,512]{1,0:T(8,128)(2,1)S(1)}, u32[]{:S(2)}, u32[]{:S(2)}) collective-permute-start(bf16[512,512]{1,0:T(8,128)(2,1)} %get-tuple-element.317), channel_id=1, source_target_pairs={{0,4},{1,5},{2,6},{3,7},{4,0},{5,1},{6,2},{7,3}} | collective-permute-start | bytes 1572872 | tf_op jit(solution)/shard_map/ppermute | solution.py:347
  1116.8 69.9 %collective-permute-start.39 = (bf16[512,512]{1,0:T(8,128)(2,1)}, bf16[512,512]{1,0:T(8,128)(2,1)S(1)}, u32[]{:S(2)}, u32[]{:S(2)}) collective-permute-start(bf16[512,512]{1,0:T(8,128)(2,1)} %get-tuple-element.316), channel_id=1, source_target_pairs={{0,5},{1,4},{2,7},{3,6},{4,1},{5,0},{6,3},{7,2}} | collective-permute-start | bytes 1572872 | tf_op jit(solution)/shard_map/ppermute | solution.py:347
  1118.2 68.5 %collective-permute-start.40 = (bf16[512,512]{1,0:T(8,128)(2,1)}, bf16[512,512]{1,0:T(8,128)(2,1)}, u32[]{:S(2)}, u32[]{:S(2)}) collective-permute-start(bf16[512,512]{1,0:T(8,128)(2,1)} %get-tuple-element.315), channel_id=1, source_target_pairs={{0,6},{1,7},{2,4},{3,5},{4,2},{5,3},{6,0},{7,1}} | collective-permute-start | bytes 1572872 | tf_op jit(solution)/shard_map/ppermute | solution.py:347
  1139.9 46.7 %collective-permute-start.41 = (bf16[512,512]{1,0:T(8,128)(2,1)}, bf16[512,512]{1,0:T(8,128)(2,1)}, u32[]{:S(2)}, u32[]{:S(2)}) collective-permute-start(bf16[512,512]{1,0:T(8,128)(2,1)} %get-tuple-element.314), channel_id=1, source_target_pairs={{0,7},{1,6},{2,5},{3,4},{4,3},{5,2},{6,1},{7,0}} | collective-permute-start | bytes 1572872 | tf_op jit(solution)/shard_map/ppermute | solution.py:347
  1227.6 4.0 collective-permute-start.57
  1231.7 4.0 collective-permute-start.58
  (41 other events, 800.4 us)
Sparse Core Ops, SparseCore 0:
  37.4 83.2 all-gather.13
  123.1 84.1 all-gather.15
  209.8 84.2 all-gather.17
  541.3 151.9 reduce-scatter.1
  854.7 143.7 all-gather.11
  1110.1 129.2 all-gather.21
  1241.2 84.1 all-gather.19
